TPU v7x, 32 devices: a whole 2x2x4 slice. The times are simulated.
32 devices in a mesh: dp: 2 (over x), tp: 4 (over z), ep: 4 (over y, core).
Axes of the slice: x: 2, y: 2, z: 4, core: 2. Of those that a mesh axis runs over, the one named last changes fastest.
Arguments:
- hidden: bfloat16 [4096, 1536], P(('dp', 'ep')), parts along dimension 0
- expert_ids: int32 [4096, 8], P(('dp', 'ep')), parts along dimension 0
- norm_w: bfloat16 [1536], replicated
- router_w: bfloat16 [1536, 40], replicated
- w_gate: bfloat16 [40, 1536, 512], P('ep', None, 'tp')
- w_up: bfloat16 [40, 1536, 512], P('ep', None, 'tp')
- w_down: bfloat16 [40, 512, 1536], P('ep', 'tp')
Outputs:
- output: bfloat16 [4096, 1536], P(('dp', 'ep')), parts along dimension 0
There are 2 independent parts. A program takes and returns all parts, laid end to end along the dimension named above; an argument that names none is the same for every part.
All inputs are finite; a program needn't handle non-finite values.
Results may differ from a plain program's by a relative error of at most 0.0113036.
Values are sent between devices in bfloat16 or wider.
A program may use at most 1 GiB of HBM per device.

v0:
```python
import jax
import jax.numpy as jnp
from jax import lax
from jax.sharding import PartitionSpec as P

NORM_EPS = 1e-6


def rms_norm(hidden, norm_w):
    wide_h = hidden.astype(jnp.float32)
    mean_sq = jnp.mean(wide_h * wide_h, axis=-1, keepdims=True)
    return (wide_h * lax.rsqrt(mean_sq + NORM_EPS) * norm_w.astype(jnp.float32)).astype(jnp.bfloat16)


def slot_rank(expert_ids, n_experts):
    flat_ids = expert_ids.reshape(-1)
    one_hot = (flat_ids[:, None] == jnp.arange(n_experts, dtype=jnp.int32)[None, :]).astype(jnp.int32)
    running = jnp.cumsum(one_hot, axis=0)
    return jnp.sum(running * one_hot, axis=1) - 1


def row_cap(tok_dev, top_k, n_experts):
    return 8 * ((2 * top_k * tok_dev + 8 * n_experts - 1) // (8 * n_experts))


def gather_slots(normed, slot_dest, n_slots, top_k):
    pair_tok = jnp.arange(slot_dest.shape[0], dtype=jnp.int32) // top_k
    src_tok = jnp.zeros((n_slots,), jnp.int32).at[slot_dest].set(pair_tok)
    filled = jnp.zeros((n_slots,), jnp.int32).at[slot_dest].set(1)
    return jnp.where(filled[:, None] > 0, normed[src_tok], jnp.zeros((), jnp.bfloat16))


def solution(mesh):
    ep_size = mesh.shape["ep"]

    def per_device(hidden, expert_ids, norm_w, router_w, w_gate, w_up, w_down):
        tok_dev, model_dim = hidden.shape
        top_k = expert_ids.shape[1]
        n_experts = router_w.shape[1]
        local_exp = w_gate.shape[0]
        row_limit = row_cap(tok_dev, top_k, n_experts)
        n_slots = n_experts * row_limit
        normed = rms_norm(hidden, norm_w)
        logits = jnp.dot(normed, router_w, preferred_element_type=jnp.float32)
        gate_prob = jnp.take_along_axis(jax.nn.softmax(logits, axis=-1), expert_ids, axis=-1)
        slot_dest = expert_ids.reshape(-1) * row_limit + slot_rank(expert_ids, n_experts)
        send_rows = gather_slots(normed, slot_dest, n_slots, top_k).reshape(ep_size, local_exp, row_limit, model_dim)
        recv_rows = lax.all_to_all(send_rows, "ep", 0, 2, tiled=True).reshape(local_exp, ep_size * row_limit, model_dim)
        gate_pre = jnp.einsum("erd,edf->erf", recv_rows, w_gate, preferred_element_type=jnp.float32)
        up_pre = jnp.einsum("erd,edf->erf", recv_rows, w_up, preferred_element_type=jnp.float32)
        act_rows = (jax.nn.silu(gate_pre) * up_pre).astype(jnp.bfloat16)
        part_out = jnp.einsum("erf,efd->erd", act_rows, w_down, preferred_element_type=jnp.float32).astype(jnp.bfloat16)
        expert_out = lax.psum(part_out, "tp")
        back_rows = lax.all_to_all(expert_out.reshape(1, local_exp, ep_size * row_limit, model_dim), "ep", 2, 0, tiled=True)
        picked = back_rows.reshape(n_slots, model_dim)[slot_dest].reshape(tok_dev, top_k, model_dim)
        moe_sum = jnp.sum(picked.astype(jnp.float32) * gate_prob[:, :, None], axis=1)
        return (hidden.astype(jnp.float32) + moe_sum).astype(jnp.bfloat16)

    token_spec = P(("dp", "ep"), None)
    return jax.shard_map(per_device, mesh=mesh, in_specs=(token_spec, token_spec, P(None), P(None, None), P("ep", None, "tp"), P("ep", None, "tp"), P("ep", "tp", None)), out_specs=token_spec, check_vma=False)
```

profile of v0, /device:TPU:0, one launch (start us, length us, event | category | flops | bytes accessed | tf_op | source)
XLA Modules:
  0.0 1886.5 jit_solution(14846647456469831957)
XLA Ops:
  6.5 0.0 copy-start
  6.5 0.0 all-reduce.2.cloned.1.call-start
  6.5 0.8 broadcast_multiply_fusion
  7.3 0.8 copy.38
  8.1 0.1 eq.29
  8.3 0.1 eq.25
  8.4 0.0 copy-start.2
  8.5 1.9 fusion.1
  10.4 0.7 convert_element_type.32
  11.1 0.1 copy.37
  11.2 0.2 mul.55
  11.4 0.1 fusion.10
  11.5 11.5 reduce-window.6
  23.0 0.2 slice.14
  23.2 0.3 copy.48
  23.5 0.2 reduce-window.9
  23.7 0.2 broadcast_add_fusion
  24.0 0.4 fusion.9
  24.5 0.0 copy-start.5
  24.5 15.5 scatter_custom_fusion.1
  40.0 15.5 scatter_custom_fusion
  55.6 0.0 copy-done.5
  55.6 0.1 broadcast_in_dim.20
  55.7 0.0 copy-done.2
  55.7 0.4 fusion.3
  56.1 28.4 %gather_fusion = bf16[8320,1536]{1,0:T(8,128)(2,1)} fusion(bf16[512,1536]{1,0:T(8,128)(2,1)S(1)} %fusion.3, s32[9216]{0:T(1024)S(1)} %pad_clamp_fusion), kind=kCustom, calls=%fused_computation | custom fusion | bytes 51151360 | tf_op jit(solution)/shard_map/gather | solution.py:30
  84.6 17.9 broadcast_select_fusion
  102.4 283.1 %all_to_all.30 = bf16[4,10,208,1536]{3,2,1,0:T(8,128)(2,1)S(1)} all-to-all(bf16[4,10,208,1536]{3,2,1,0:T(8,128)(2,1)} %broadcast_select_fusion), channel_id=1, replica_groups=mesh['dp'=2,'tp'=4,'ep'=4] {'ep'}, dimensions={0} | all-to-all | bytes 51118080 | tf_op jit(solution)/shard_map/all_to_all | solution.py:48
  385.5 0.0 copy-start.7
  385.5 9.2 copy.42
  394.8 0.0 copy-done.7
  394.8 13.9 fusion.22
  408.6 26.4 %convert_bitcast_fusion = bf16[1,10,832,1536]{3,2,1,0:T(8,128)(2,1)} fusion(bf16[10,128,1536]{2,1,0:T(8,128)(2,1)} %param.13, f32[10,832,128]{2,1,0:T(8,128)} %fusion.22, bf16[10,832,1536]{2,1,0:T(8,128)(2,1)} %bitcast.49, bf16[10,1536,128]{2,1,0:T(8,128)(2,1)} %param.12), kind=kOutput, calls=%fused_computation.5 | convolution fusion | flops 6562283520 | bytes 63242240 | tf_op jit(solution)/shard_map/erf,efd->erd/dot_general | solution.py:52
  435.0 0.0 all-reduce.2.cloned.1.call-update
  435.0 842.9 %all-reduce.2.cloned.1.call-done = bf16[1,10,832,1536]{3,2,1,0:T(8,128)(2,1)} async-done(((bf16[1,10,832,1536]{3,2,1,0:T(8,128)(2,1)}), bf16[1,10,832,1536]{3,2,1,0:T(8,128)(2,1)}) %all-reduce.2.cloned.1.call-update) | async-done | bytes 25559056 | tf_op jit(solution)/shard_map/psum | solution.py:53
  1277.9 51.9 %copy.43 = bf16[1,10,832,1536]{3,1,0,2:T(8,128)(2,1)} copy(bf16[1,10,832,1536]{3,2,1,0:T(8,128)(2,1)} %all-reduce.2.cloned.1.call-done) | data formatting | bytes 51118080 | tf_op jit(solution)/shard_map/psum | solution.py:53
  1329.8 0.0 copy-start.4
  1329.8 11.4 all-to-all-start.1
  1341.1 0.0 copy-done.4
  1341.2 0.1 copy.45
  1341.3 0.2 reshape.118
  1341.5 0.0 copy-done
  1341.5 0.6 fusion.21
  1342.1 0.0 copy-start.6
  1342.1 33.0 %gather_fusion.2 = f32[4096]{0:T(1024)S(1)} fusion(f32[512,40]{0,1:T(8,128)S(1)} %fusion.11, s32[4096]{0:T(1024)S(1)} %reshape.118), kind=kCustom, calls=%fused_computation.2 | custom fusion | bytes 65536 | tf_op jit(solution)/shard_map/jit(take_along_axis)/gather | solution.py:45
  1375.2 0.2 reshape.121
  1375.3 0.1 copy.46
  1375.4 0.1 copy.47
  1375.6 0.0 copy-done.6
  1375.6 406.4 %all-to-all-done.1 = bf16[1,10,832,1536]{3,1,0,2:T(8,128)(2,1)} async-done(((bf16[1,10,832,1536]{3,1,0,2:T(8,128)(2,1)}), bf16[1,10,832,1536]{3,1,0,2:T(8,128)(2,1)}, u32[]{:S(2)}, u32[]{:S(2)}) %all-to-all-start.1) | async-done | bytes 25559072 | tf_op jit(solution)/shard_map/all_to_all | solution.py:54
  1782.0 29.5 %copy.44 = bf16[1,10,4,208,1536]{4,3,1,2,0:T(8,128)(2,1)} copy(bf16[1,10,4,208,1536]{4,1,3,2,0:T(8,128)(2,1)} %bitcast.10) | data formatting | bytes 51118080 | tf_op jit(solution)/shard_map/all_to_all | solution.py:54
  1811.5 36.9 %gather_fusion.1 = bf16[4096,1536]{1,0:T(8,128)(2,1)} fusion(bf16[8320,1536]{1,0:T(8,128)(2,1)} %bitcast.45, s32[4096]{0:T(1024)S(1)} %broadcast_clamp_fusion), kind=kCustom, calls=%fused_computation.1 | custom fusion | bytes 25182208 | tf_op jit(solution)/shard_map/gather | solution.py:55
  1848.4 0.0 copy-start.3
  1848.4 0.0 copy-start.1
  1848.4 29.6 %fusion = f32[512,1536]{1,0:T(8,128)S(1)} fusion(bf16[4096,1536]{1,0:T(8,128)(2,1)} %gather_fusion.1, f32[512,8]{1,0:T(8,128)S(1)} %copy.47), kind=kLoop, calls=%fused_computation.8 | loop fusion | flops 18087936 | bytes 15745024 | tf_op jit(solution)/shard_map/reduce_sum | solution.py:56
  1878.0 0.0 copy-done.3
  1878.0 1.6 fusion.4
  1879.6 0.0 copy-done.1
  (13 shorter events, 0.2 us)
Async XLA Ops:
  6.5 1334.9 %copy-start = (bf16[1536,40]{0,1:T(8,128)(2,1)S(1)}, bf16[1536,40]{0,1:T(8,128)(2,1)}, u32[]{:S(2)}) copy-start(bf16[1536,40]{0,1:T(8,128)(2,1)} %param.10) | copy-start | bytes 368644
  6.5 1271.4 %all-reduce.2.cloned.1.call-start = ((), (), s32[]{:S(2)}) async-start(), calls=%async_computation.2 | async-start | bytes 51118080 | tf_op jit(solution)/shard_map/psum | solution.py:53
  8.4 47.3 %copy-start.2 = (bf16[512,1536]{1,0:T(8,128)(2,1)S(1)}, bf16[512,1536]{1,0:T(8,128)(2,1)}, u32[]{:S(2)}) copy-start(bf16[512,1536]{1,0:T(8,128)(2,1)} %param.7) | copy-start | bytes 4718596
  24.5 31.1 %copy-start.5 = (s32[4096,1]{0,1:T(1,128)}, s32[4096,1]{0,1:T(1,128)S(1)}, u32[]{:S(2)}) copy-start(s32[4096,1]{0,1:T(1,128)S(1)} %compare_select_fusion.1) | copy-start | bytes 49156
  385.5 9.2 copy-start.7
  1329.8 11.4 copy-start.4
  1329.8 452.3 %all-to-all-start.1 = ((bf16[1,10,832,1536]{3,1,0,2:T(8,128)(2,1)}), bf16[1,10,832,1536]{3,1,0,2:T(8,128)(2,1)}, u32[]{:S(2)}, u32[]{:S(2)}) async-start(bf16[1,10,832,1536]{3,1,0,2:T(8,128)(2,1)} %copy.43), calls=%async_computation.1 | async-start | bytes 81788928 | tf_op jit(solution)/shard_map/all_to_all | solution.py:54
  1342.1 33.5 %copy-start.6 = (s32[4096,1]{0,1:T(1,128)S(1)}, s32[4096,1]{0,1:T(1,128)}, u32[]{:S(2)}) copy-start(s32[4096,1]{0,1:T(1,128)} %copy-done.5) | copy-start | bytes 49156
  1848.4 29.6 %copy-start.3 = (bf16[512,1536]{1,0:T(8,128)(2,1)S(1)}, bf16[512,1536]{1,0:T(8,128)(2,1)}, u32[]{:S(2)}) copy-start(bf16[512,1536]{1,0:T(8,128)(2,1)} %param.7) | copy-start | bytes 4718596
  1848.4 31.2 %copy-start.1 = (bf16[1536,40]{0,1:T(8,128)(2,1)S(1)}, bf16[1536,40]{0,1:T(8,128)(2,1)}, u32[]{:S(2)}) copy-start(bf16[1536,40]{0,1:T(8,128)(2,1)} %param.10) | copy-start | bytes 368644
Sparse Core Ops, SparseCore 0:
  435.1 842.7 all-reduce.1
where the time goes:
time: 1890 us
  waiting for transfers between devices  1250 us (66%)
  blocking collectives  283 us (15%)
  local copies, waits for them, and re-layouts  223 us (12%)
  other arithmetic  65.4 us (3%)
  matrix products  40.8 us (2%)
    psum x1, waiting for transfers between devices, per_device(): expert_out = lax.psum(part_out, 'tp')  843 us
    all_to_all x1, waiting for transfers between devices, per_device(): lax.all_to_all(expert_out.reshape(1, local_exp, ep_size * row_limit, mode...  406 us
    all_to_all x1, blocking collectives, per_device(): lax.all_to_all(send_rows, 'ep', 0, 2, tiled=True)  283 us
    psum x1, local copies, waits for them, and re-layouts, per_device(): expert_out = lax.psum(part_out, 'tp')  51.9 us
  transfers between devices with their start and end apart: 2, of which 2 were waited for; matrix products, arithmetic and copies ran while one was open for 2% of the time, Pallas kernels for 0%

commit v1 on v0

v1 whole, which is shorter than its diff:
```python
import jax
import jax.numpy as jnp
from jax import lax
from jax.sharding import PartitionSpec as P

NORM_EPS = 1e-6


def rms_norm(hidden, norm_w):
    wide_h = hidden.astype(jnp.float32)
    mean_sq = jnp.mean(wide_h * wide_h, axis=-1, keepdims=True)
    return (wide_h * lax.rsqrt(mean_sq + NORM_EPS) * norm_w.astype(jnp.float32)).astype(jnp.bfloat16)


def solution(mesh):
    def per_device(hidden, expert_ids, norm_w, router_w, w_gate, w_up, w_down):
        tok_dev, model_dim = hidden.shape
        n_experts = router_w.shape[1]
        local_exp, _, width = w_gate.shape
        normed = rms_norm(hidden, norm_w)
        logits = jnp.dot(normed, router_w, preferred_element_type=jnp.float32)
        prob = jax.nn.softmax(logits, axis=-1)
        chosen = jnp.any(expert_ids[:, :, None] == jnp.arange(n_experts, dtype=jnp.int32)[None, None, :], axis=1)
        gates = jnp.where(chosen, prob, 0.0)
        all_rows = lax.all_gather(normed, "ep", axis=0, tiled=True)
        all_gates = lax.all_gather(gates, "ep", axis=0, tiled=True)
        my_gates = lax.dynamic_slice_in_dim(all_gates, lax.axis_index("ep") * local_exp, local_exp, axis=1)
        gate_pre = jnp.einsum("td,edf->etf", all_rows, w_gate, preferred_element_type=jnp.float32)
        up_pre = jnp.einsum("td,edf->etf", all_rows, w_up, preferred_element_type=jnp.float32)
        act = (jax.nn.silu(gate_pre) * up_pre).astype(jnp.bfloat16).astype(jnp.float32)
        act = (act * my_gates.T[:, :, None]).astype(jnp.bfloat16)
        part = jnp.einsum("etf,efd->td", act, w_down, preferred_element_type=jnp.float32).astype(jnp.bfloat16)
        mine = lax.psum_scatter(part, "ep", scatter_dimension=0, tiled=True)
        total = lax.psum(mine, "tp")
        return (hidden.astype(jnp.float32) + total.astype(jnp.float32)).astype(jnp.bfloat16)

    token_spec = P(("dp", "ep"), None)
    return jax.shard_map(per_device, mesh=mesh, in_specs=(token_spec, token_spec, P(None), P(None, None), P("ep", None, "tp"), P("ep", None, "tp"), P("ep", "tp", None)), out_specs=token_spec, check_vma=False)
```

time: 1890 us -> 240 us (0.13)
  waiting for transfers between devices: 1250 us -> 168 us
  blocking collectives: 283 us -> 7.64 us
  local copies, waits for them, and re-layouts: 223 us -> 0.03 us
  other arithmetic: 65.4 us -> 8.61 us
    psum x1, waiting for transfers between devices: 843 us -> 71.2 us  [per_device(): total = lax.psum(mine, 'tp')]
    all_to_all x1 -> x0, waiting for transfers between devices: 406 us -> none  [per_device(): lax.all_to_all(expert_out.reshape(1, local_exp, ep_size * row_limit, mode...]
    all_to_all x1 -> x0, blocking collectives: 283 us -> none  [per_device(): lax.all_to_all(send_rows, 'ep', 0, 2, tiled=True)]
    gather x7 -> x0, local copies, waits for them, and re-layouts: 98.9 us -> none  [the longest x1 36.9 us: per_device(): back_rows.reshape(n_slots, model_dim)[slot_dest]]
    reduce_scatter x0 -> x1, waiting for transfers between devices: none -> 57 us  [per_device(): mine = lax.psum_scatter(part, 'ep', scatter_dimension=0, tiled=True)]
    psum x1 -> x0, local copies, waits for them, and re-layouts: 51.9 us -> none  [per_device(): expert_out = lax.psum(part_out, 'tp')]
    all_gather x0 -> x1, waiting for transfers between devices: none -> 39.4 us  [per_device(): all_rows = lax.all_gather(normed, 'ep', axis=0, tiled=True)]
    all_to_all x2 -> x0, local copies, waits for them, and re-layouts: 38.7 us -> none  [the longest x1 29.5 us: per_device(): lax.all_to_all(expert_out.reshape(1, local_exp, ep_size * row_limit, mode...]
  transfers between devices with their start and end apart: 2 -> 3, of which waited for: 2 -> 3; matrix products, arithmetic and copies ran while one was open for 2% -> 1% of each run, Pallas kernels for 0% -> 0%
where the time goes in v1:
time: 240 us
  waiting for transfers between devices  168 us (70%)
  matrix products  43 us (18%)
  between operations  13.2 us (6%)
  other arithmetic  8.61 us (4%)
  blocking collectives  7.64 us (3%)
    psum x1, waiting for transfers between devices, per_device(): total = lax.psum(mine, 'tp')  71.2 us
    reduce_scatter x1, waiting for transfers between devices, per_device(): mine = lax.psum_scatter(part, 'ep', scatter_dimension=0, tiled=True)  57 us
    all_gather x1, waiting for transfers between devices, per_device(): all_rows = lax.all_gather(normed, 'ep', axis=0, tiled=True)  39.4 us
    dot_general x1, matrix products, per_device(): jnp.einsum('etf,efd->td', act, w_down, preferred_element_type=jnp.float32)  27.1 us
    dot_general x1, matrix products, per_device(): jnp.einsum('td,edf->etf', all_rows, w_up, preferred_element_type=jnp.floa...  14 us
    all_gather x1, blocking collectives, per_device(): all_gates = lax.all_gather(gates, 'ep', axis=0, tiled=True)  7.64 us
  transfers between devices with their start and end apart: 3, of which 3 were waited for; matrix products, arithmetic and copies ran while one was open for 1% of the time, Pallas kernels for 0%

profile of v1, /device:TPU:0, one launch (start us, length us, event | category | flops | bytes accessed | tf_op | source)
XLA Modules:
  0.0 240.1 jit_solution(9934514647057856604)
XLA Ops:
  6.5 0.0 copy-start
  6.5 0.0 copy-start.2
  6.5 0.0 all-gather.2.cloned.1.call-start
  6.5 1.8 fusion.11
  8.4 0.7 convert_element_type.29
  9.1 3.0 %fusion.13 = bf16[512,1536]{1,0:T(8,128)(2,1)} fusion(bf16[512,1536]{1,0:T(8,128)(2,1)} %param.7, f32[1536]{0:T(1024)S(1)} %convert_element_type.29, f32[512]{0:T(512)S(1)} %add_rsqrt_fusion), kind=kLoop, calls=%fused_computation.19 | loop fusion | flops 3145728 | bytes 3153920 | tf_op jit(solution)/shard_map/convert_element_type | solution.py:12
  12.0 0.0 all-gather.2.cloned.1.call-update
  12.1 0.0 reduce-scatter.2.cloned.1.call-start
  12.1 0.0 copy-done
  12.1 2.0 fusion.22
  14.2 0.0 copy-done.2
  14.2 0.1 fusion.19
  14.3 7.6 %all_gather.7 = f32[2048,40]{0,1:T(8,128)S(1)} all-gather(f32[512,40]{0,1:T(8,128)S(1)} %divide_select_fusion), channel_id=1, replica_groups=mesh['dp'=2,'tp'=4,'ep'=4] {'ep'}, dimensions={0}, use_global_device_ids=true | all-gather | bytes 409600 | tf_op jit(solution)/shard_map/all_gather | solution.py:26
  22.0 39.4 %all-gather.2.cloned.1.call-done = bf16[2048,1536]{1,0:T(8,128)(2,1)} async-done(((bf16[512,1536]{1,0:T(8,128)(2,1)}), bf16[2048,1536]{1,0:T(8,128)(2,1)}) %all-gather.2.cloned.1.call-update) | async-done | bytes 6291472 | tf_op jit(solution)/shard_map/all_gather | solution.py:25
  61.4 14.0 %fusion.4 = f32[2048,10,128]{2,0,1:T(8,128)} fusion(bf16[10,1536,128]{2,1,0:T(8,128)(2,1)} %param.12, bf16[2048,1536]{1,0:T(8,128)(2,1)} %all-gather.2.cloned.1.call-done), kind=kOutput, calls=%fused_computation.9 | convolution fusion | flops 8053063680 | bytes 20709376 | tf_op jit(solution)/shard_map/td,edf->etf/dot_general | solution.py:29
  75.3 27.1 %bitcast_convert_fusion = bf16[2048,1536]{1,0:T(8,128)(2,1)} fusion(bf16[10,128,1536]{2,1,0:T(8,128)(2,1)} %param.13, f32[10,2048]{1,0:T(8,128)S(1)} %dynamic-slice_bitcast_fusion, f32[2048,10,128]{2,0,1:T(8,128)} %fusion.4, bf16[10,1536,128]{2,1,0:T(8,128)(2,1)} %param.11, bf16[2048,1536]{1,0:T(8,128)(2,1)} %all-gather.2.cloned.1.call-done), kind=kOutput, calls=%fused_computation | convolution fusion | flops 16132866048 | bytes 31014912 | tf_op jit(solution)/shard_map/etf,efd->td/dot_general | solution.py:32
  102.4 0.0 copy-start.1
  102.4 0.0 reduce-scatter.2.cloned.1.call-update
  102.4 0.0 all-reduce.2.cloned.1.call-start
  102.5 57.0 %reduce-scatter.2.cloned.1.call-done = bf16[512,1536]{1,0:T(8,128)(2,1)} async-done(((bf16[2048,1536]{1,0:T(8,128)(2,1)}), bf16[512,1536]{1,0:T(8,128)(2,1)}) %reduce-scatter.2.cloned.1.call-update) | async-done | bytes 1572880 | tf_op jit(solution)/shard_map/reduce_scatter | solution.py:33
  159.4 0.0 all-reduce.2.cloned.1.call-update
  159.4 71.2 %all-reduce.2.cloned.1.call-done = bf16[512,1536]{1,0:T(8,128)(2,1)} async-done(((bf16[512,1536]{1,0:T(8,128)(2,1)}), bf16[512,1536]{1,0:T(8,128)(2,1)}) %all-reduce.2.cloned.1.call-update) | async-done | bytes 1572880 | tf_op jit(solution)/shard_map/psum | solution.py:34
  230.6 0.0 copy-done.1
  230.6 2.9 %fusion.14 = bf16[512,1536]{1,0:T(8,128)(2,1)} fusion(bf16[512,1536]{1,0:T(8,128)(2,1)S(1)} %copy-done.1, bf16[512,1536]{1,0:T(8,128)(2,1)} %all-reduce.2.cloned.1.call-done), kind=kLoop, calls=%fused_computation.20 | loop fusion | flops 3145728 | bytes 4718592 | tf_op jit(solution)/shard_map/convert_element_type | solution.py:35
  (4 shorter events, 0.1 us)
Async XLA Ops:
  6.5 5.6 %copy-start = (bf16[1536,40]{0,1:T(8,128)(2,1)S(1)}, bf16[1536,40]{0,1:T(8,128)(2,1)}, u32[]{:S(2)}) copy-start(bf16[1536,40]{0,1:T(8,128)(2,1)} %param.10) | copy-start | bytes 368644
  6.5 7.6 %copy-start.2 = (s32[512,8]{0,1:T(8,128)S(1)}, s32[512,8]{0,1:T(8,128)}, u32[]{:S(2)}) copy-start(s32[512,8]{0,1:T(8,128)} %param.8) | copy-start | bytes 49156
  6.5 54.8 %all-gather.2.cloned.1.call-start = ((), (), s32[]{:S(2)}) async-start(), calls=%async_computation.1 | async-start | bytes 7864320 | tf_op jit(solution)/shard_map/all_gather | solution.py:25
  12.1 147.4 %reduce-scatter.2.cloned.1.call-start = ((), (), s32[]{:S(2)}) async-start(), calls=%async_computation.2 | async-start | bytes 7864320 | tf_op jit(solution)/shard_map/reduce_scatter | solution.py:33
  102.4 128.3 %copy-start.1 = (bf16[512,1536]{1,0:T(8,128)(2,1)S(1)}, bf16[512,1536]{1,0:T(8,128)(2,1)}, u32[]{:S(2)}) copy-start(bf16[512,1536]{1,0:T(8,128)(2,1)} %param.7) | copy-start | bytes 4718596
  102.4 128.2 %all-reduce.2.cloned.1.call-start = ((), (), s32[]{:S(2)}) async-start(), calls=%async_computation.3 | async-start | bytes 3145728 | tf_op jit(solution)/shard_map/psum | solution.py:34
Sparse Core Ops, SparseCore 0:
  12.2 49.1 all-gather.1
  102.5 56.8 reduce-scatter.1
  161.8 68.7 all-reduce.1

commit v2 on v1

v2 whole, which is shorter than its diff:
```python
import functools

import jax
import jax.numpy as jnp
from jax import lax
from jax.experimental import pallas as pl
from jax.experimental.pallas import tpu as pltpu
from jax.sharding import PartitionSpec as P

NORM_EPS = 1e-6
MESH = pl.DeviceIdType.MESH
OWN_SLOT = (0, 1, 2, 5)
FAR_SLOT = (3, 4, 6, 7)
N_SUB = 4
PIECE = 32


def body(n_experts, ids_ref, h_ref, nw_ref, wr_ref, wg_hbm, wu_hbm, wd_hbm, out_hbm,
         v, wgu, wd, act, keep, dsend, drecv, sbuf, rbuf, tbuf, abuf, ubuf, obuf, ids_all, ids_slot,
         w_sem, ids_s, ids_r, d1_s, d1_r, dy_s, dy_r, dz_s, dz_r, dd_s, dd_r, pd_s, pd_r,
         sy_s, sy_r, ra_s, ra_r, rb_s, rb_r, rc_s, rc_r, o_sem):
    tok, dim = h_ref.shape
    local_exp, _, width = wg_hbm.shape
    sub = tok // N_SUB
    half = sub // 2
    n_piece = tok // PIECE
    per_sub = sub // PIECE
    ep = lax.axis_index("ep")
    z = lax.axis_index("tp")
    core, y = ep % 2, ep // 2
    ep_pair = 2 * y + 1 - core
    ep_far = 2 * (1 - y) + core
    ep_diag = 2 * (1 - y) + 1 - core
    side = z % 2
    z_pair = z + 1 - 2 * side
    z_mirror = 3 - z
    inner = jnp.logical_or(z == 1, z == 2)
    outer = jnp.logical_or(z == 0, z == 3)

    def remote(src, dst, ssem, rsem, **where):
        return pltpu.make_async_remote_copy(src_ref=src, dst_ref=dst, send_sem=ssem, recv_sem=rsem, device_id=where, device_id_type=MESH)

    def weight_copies():
        copies = []
        for e in range(local_exp):
            copies.append(pltpu.make_async_copy(wg_hbm.at[e], wgu.at[e, :, pl.ds(0, width)], w_sem.at[2 * e]))
            copies.append(pltpu.make_async_copy(wu_hbm.at[e], wgu.at[e, :, pl.ds(width, width)], w_sem.at[2 * e + 1]))
        copies.append(pltpu.make_async_copy(wd_hbm, wd, w_sem.at[2 * local_exp]))
        return copies

    barrier = pltpu.get_barrier_semaphore()
    for where in ({"ep": ep_pair}, {"ep": ep_far}, {"ep": ep_diag}, {"tp": z_pair}, {"tp": z_mirror}):
        pl.semaphore_signal(barrier, inc=1, device_id=where, device_id_type=MESH)
    for copy in weight_copies():
        copy.start()

    def norm_rows(s):
        slot = OWN_SLOT[s]

        def group(i, carry):
            r = pl.multiple_of(i * 16, 16)
            x = h_ref[pl.ds(s * sub + r, 16), :].astype(jnp.float32)
            ms = jnp.mean(x * x, axis=-1, keepdims=True)
            v[slot, pl.ds(r, 16), :] = (x * lax.rsqrt(ms + NORM_EPS) * nw_ref[...].astype(jnp.float32)).astype(jnp.bfloat16)
            return carry

        lax.fori_loop(0, sub // 16, group, 0)

    def half_rows(which):
        return pl.ds(pl.multiple_of(which * half, half), half)

    def ids_copy(k):
        ep_to = (ep_pair, ep_far, ep_diag)[k]
        return remote(ids_ref, ids_all.at[k], ids_s.at[k], ids_r.at[k], ep=ep_to)

    def d1(s):
        slot = OWN_SLOT[s]
        return remote(v.at[slot, pl.ds(0, sub)], v.at[slot, pl.ds(sub, sub)], d1_s.at[s], d1_r.at[s], ep=ep_pair)

    def dy(s):
        rows = half_rows(side)
        return remote(v.at[OWN_SLOT[s], rows], v.at[FAR_SLOT[s], rows], dy_s.at[s], dy_r.at[s], ep=ep_far)

    def dz(s):
        rows = half_rows(side)
        return remote(v.at[FAR_SLOT[s], rows], v.at[FAR_SLOT[s], rows], dz_s.at[s], dz_r.at[s], tp=z_pair)

    def dz_in(s):
        rows = half_rows(1 - side)
        return remote(v.at[FAR_SLOT[s], rows], v.at[FAR_SLOT[s], rows], dz_s.at[s], dz_r.at[s], tp=z_pair)

    def dd(s, k):
        which = side if k == 0 else 1 - side
        src = pl.ds(pl.multiple_of(which * half, half), half)
        dst = pl.ds(pl.multiple_of(sub + which * half, half), half)
        return remote(v.at[FAR_SLOT[s], src], v.at[FAR_SLOT[s], dst], dd_s.at[2 * s + k], dd_r.at[2 * s + k], ep=ep_pair)

    def pd(slot):
        return remote(dsend.at[slot], drecv.at[slot], pd_s.at[slot], pd_r.at[slot], ep=ep_pair)

    def piece_rows(p):
        return pl.ds(pl.multiple_of(p * PIECE, PIECE), PIECE)

    def sy(p):
        return remote(sbuf.at[piece_rows(p)], rbuf.at[piece_rows(p)], sy_s.at[p], sy_r.at[p], ep=ep_far)

    def ra(p):
        return remote(tbuf.at[piece_rows(p)], abuf.at[piece_rows(p)], ra_s.at[p], ra_r.at[p], tp=z_pair)

    def rb(p):
        return remote(tbuf.at[piece_rows(p)], ubuf.at[piece_rows(p)], rb_s.at[p], rb_r.at[p], tp=z_mirror)

    def rc(p):
        return remote(obuf.at[piece_rows(p)], obuf.at[piece_rows(p)], rc_s.at[p], rc_r.at[p], tp=z_pair)

    def out_copy(p):
        return pltpu.make_async_copy(obuf.at[piece_rows(p)], out_hbm.at[piece_rows(p)], o_sem.at[p])

    norm_rows(0)
    pl.semaphore_wait(barrier, 5)
    for s in range(N_SUB):
        if s:
            norm_rows(s)
        dy(s).start()
        d1(s).start()
        if s == 0:
            for k in range(3):
                ids_copy(k).start()

    def far_in(s):
        dy(s).wait_recv()
        dz(s).start()
        dd(s, 0).start()

    def far_pair_in(s):
        dz_in(s).wait_recv()
        dd(s, 1).start()

    def far_ready(s):
        dd(s, 0).wait_recv()
        dd(s, 1).wait_recv()

    def ids_own():
        ids_copy(0).wait_recv()
        for s in range(N_SUB):
            ids_slot[OWN_SLOT[s], 0] = ids_ref[s]
            ids_slot[OWN_SLOT[s], 1] = ids_all[0, s]

    def ids_far():
        ids_copy(1).wait_recv()
        ids_copy(2).wait_recv()
        for s in range(N_SUB):
            ids_slot[FAR_SLOT[s], 0] = ids_all[1, s]
            ids_slot[FAR_SLOT[s], 1] = ids_all[2, s]

    def far_sum(s):
        slot = FAR_SLOT[s]
        pd(slot).wait_recv()

        def one(i, carry):
            r = pl.multiple_of(i * PIECE, PIECE)
            total = keep[slot, pl.ds(r, PIECE), :] + drecv[slot, pl.ds(r, PIECE), :].astype(jnp.float32)
            sbuf[pl.ds(s * sub + r, PIECE), :] = total.astype(jnp.bfloat16)
            sy(s * per_sub + i).start()
            return carry

        lax.fori_loop(0, per_sub, one, 0)

    for copy in weight_copies():
        copy.wait()

    pre = {0: [lambda: d1(0).wait_recv(), ids_own],
           1: [lambda: d1(1).wait_recv()],
           2: [lambda: d1(2).wait_recv()],
           3: [lambda: far_pair_in(0), ids_far, lambda: far_ready(0)],
           4: [lambda: far_ready(1)],
           5: [lambda: d1(3).wait_recv()],
           6: [lambda: far_pair_in(3), lambda: far_ready(2)],
           7: [lambda: far_ready(3)]}
    mid = {1: [lambda: far_in(0)],
           2: [lambda: far_in(1)],
           3: [lambda: far_in(2), lambda: far_pair_in(1)],
           4: [lambda: far_in(3), lambda: far_sum(0)],
           5: [lambda: far_pair_in(2), lambda: far_sum(1)],
           7: [lambda: far_sum(2)]}

    def run(tasks, step):
        for k, fns in tasks.items():
            @pl.when(step == k)
            def _(fns=fns):
                for fn in fns:
                    fn()

    def chosen_of(tile):
        expert = lax.broadcasted_iota(jnp.int32, (16, sub), 0) + ep * local_exp
        hit = jnp.zeros((16, sub), jnp.float32)
        for j in range(tile.shape[0]):
            hit = jnp.where(tile[j:j + 1, :] == expert, 1.0, hit)
        full = jnp.concatenate([hit, jnp.zeros((sub - 16, sub), jnp.float32)], axis=0)
        return full.T

    @pl.loop(0, 2 * N_SUB)
    def _(step):
        run(pre, step)
        x = v.at[step]
        logits = jnp.dot(x[...], wr_ref[...], preferred_element_type=jnp.float32)
        lane = lax.broadcasted_iota(jnp.int32, logits.shape, 1)
        logits = jnp.where(lane < n_experts, logits, -jnp.inf)
        raised = jnp.exp(logits - jnp.max(logits, axis=-1, keepdims=True))
        prob = raised / jnp.sum(raised, axis=-1, keepdims=True)
        chosen = jnp.concatenate([chosen_of(ids_slot[step, 0]), chosen_of(ids_slot[step, 1])], axis=0)
        gates = prob * chosen
        for e in range(local_exp):
            gu = jnp.dot(x[...], wgu[e], preferred_element_type=jnp.float32)
            a = (jax.nn.silu(gu[:, :width]) * gu[:, width:]).astype(jnp.bfloat16).astype(jnp.float32)
            act[:, e * width:(e + 1) * width] = (a * gates[:, e:e + 1]).astype(jnp.bfloat16)
        run(mid, step)
        cols = 512
        for n in range(dim // cols):
            part = jnp.dot(act[...], wd[:, n * cols:(n + 1) * cols], preferred_element_type=jnp.float32)
            keep[step, :, n * cols:(n + 1) * cols] = part[:sub]
            dsend[step, :, n * cols:(n + 1) * cols] = part[sub:].astype(jnp.bfloat16)
        pd(step).start()

    far_sum(3)
    for s in range(N_SUB):
        pd(OWN_SLOT[s]).wait_recv()

    def stage_b(p):
        rb(p).wait_recv()
        rows = piece_rows(p)
        total = tbuf[rows, :].astype(jnp.float32) + ubuf[rows, :].astype(jnp.float32)
        obuf[rows, :] = (h_ref[rows, :].astype(jnp.float32) + total).astype(jnp.bfloat16)
        rc(p).start()
        out_copy(p).start()

    @pl.loop(0, n_piece)
    def _(p):
        s = p // per_sub
        slot = s + 2 * (s // 3)
        rows = piece_rows(p)
        in_slot = pl.ds(pl.multiple_of((p - s * per_sub) * PIECE, PIECE), PIECE)
        sy(p).wait_recv()
        total = keep[slot, in_slot, :] + drecv[slot, in_slot, :].astype(jnp.float32) + rbuf[rows, :].astype(jnp.float32)

        @pl.when(outer)
        def _():
            tbuf[rows, :] = total.astype(jnp.bfloat16)
            ra(p).start()

        @pl.when(inner)
        def _():
            ra(p).wait_recv()
            tbuf[rows, :] = (total + abuf[rows, :].astype(jnp.float32)).astype(jnp.bfloat16)
            rb(p).start()

            @pl.when(p > 0)
            def _():
                stage_b(p - 1)

    @pl.when(inner)
    def _():
        stage_b(n_piece - 1)

    @pl.when(outer)
    def _():
        @pl.loop(0, n_piece)
        def _(p):
            rc(p).wait_recv()
            out_copy(p).start()

    for k in range(3):
        ids_copy(k).wait_send()
    for s in range(N_SUB):
        d1(s).wait_send()
        dy(s).wait_send()
        dz(s).wait_send()
        dd(s, 0).wait_send()
        dd(s, 1).wait_send()

    @pl.loop(0, 2 * N_SUB)
    def _(slot):
        pd(slot).wait_send()

    @pl.loop(0, n_piece)
    def _(p):
        sy(p).wait_send()
        out_copy(p).wait()

        @pl.when(outer)
        def _():
            ra(p).wait_send()

        @pl.when(inner)
        def _():
            rb(p).wait_send()
            rc(p).wait_send()


def solution(mesh):
    def per_device(hidden, expert_ids, norm_w, router_w, w_gate, w_up, w_down):
        tok, dim = hidden.shape
        top_k = expert_ids.shape[1]
        n_experts = router_w.shape[1]
        local_exp, _, width = w_gate.shape
        sub = tok // N_SUB
        n_piece = tok // PIECE
        my_first = lax.axis_index("ep") * local_exp
        doubled = jnp.concatenate([router_w, router_w], axis=1)
        turned = lax.dynamic_slice_in_dim(doubled, my_first, n_experts, axis=1)
        turned = jnp.pad(turned, ((0, 0), (0, 128 - n_experts)))
        ids_t = expert_ids.reshape(N_SUB, sub, top_k).transpose(0, 2, 1)
        bf, f32 = jnp.bfloat16, jnp.float32
        vmem = pl.BlockSpec(memory_space=pltpu.VMEM)
        hbm = pl.BlockSpec(memory_space=pl.ANY)
        dma = pltpu.SemaphoreType.DMA
        scratch = [
            pltpu.VMEM((2 * N_SUB, 2 * sub, dim), bf),
            pltpu.VMEM((local_exp, dim, 2 * width), bf),
            pltpu.VMEM((local_exp * width, dim), bf),
            pltpu.VMEM((2 * sub, local_exp * width), bf),
            pltpu.VMEM((2 * N_SUB, sub, dim), f32),
            pltpu.VMEM((2 * N_SUB, sub, dim), bf),
            pltpu.VMEM((2 * N_SUB, sub, dim), bf),
            pltpu.VMEM((tok, dim), bf),
            pltpu.VMEM((tok, dim), bf),
            pltpu.VMEM((tok, dim), bf),
            pltpu.VMEM((tok, dim), bf),
            pltpu.VMEM((tok, dim), bf),
            pltpu.VMEM((tok, dim), bf),
            pltpu.VMEM((3, N_SUB, top_k, sub), jnp.int32),
            pltpu.VMEM((2 * N_SUB, 2, top_k, sub), jnp.int32),
            dma((2 * local_exp + 1,)),
            dma((3,)), dma((3,)),
            dma((N_SUB,)), dma((N_SUB,)),
            dma((N_SUB,)), dma((N_SUB,)),
            dma((N_SUB,)), dma((N_SUB,)),
            dma((2 * N_SUB,)), dma((2 * N_SUB,)),
            dma((2 * N_SUB,)), dma((2 * N_SUB,)),
            dma((n_piece,)), dma((n_piece,)),
            dma((n_piece,)), dma((n_piece,)),
            dma((n_piece,)), dma((n_piece,)),
            dma((n_piece,)), dma((n_piece,)),
            dma((n_piece,)),
        ]
        return pl.pallas_call(
            functools.partial(body, n_experts),
            out_shape=jax.ShapeDtypeStruct((tok, dim), bf),
            in_specs=[vmem, vmem, vmem, vmem, hbm, hbm, hbm],
            out_specs=hbm,
            scratch_shapes=scratch,
            compiler_params=pltpu.CompilerParams(collective_id=0, has_side_effects=True, vmem_limit_bytes=64_000_000),
            name="moe_layer",
        )(ids_t, hidden, norm_w.reshape(1, dim), turned, w_gate, w_up, w_down.reshape(local_exp * width, dim))

    token_spec = P(("dp", "ep"), None)
    return jax.shard_map(per_device, mesh=mesh, in_specs=(token_spec, token_spec, P(None), P(None, None), P("ep", None, "tp"), P("ep", None, "tp"), P("ep", "tp", None)), out_specs=token_spec, check_vma=False)
```

time: 240 us -> 98 us (0.41)
  waiting for transfers between devices: 168 us -> 0 us
  Pallas kernels: 0 us -> 91.4 us
  matrix products: 43 us -> 0 us
  between operations: 13.2 us -> 0.02 us
  other arithmetic: 8.61 us -> 0.44 us
  blocking collectives: 7.64 us -> 0 us
  local copies, waits for them, and re-layouts: 0.03 us -> 5.88 us
    pallas_call x0 -> x1, Pallas kernels: none -> 91.4 us  [per_device(): pl.pallas_call(functools.partial(body, n_experts), out_shape=jax.ShapeDty...]
    psum x1 -> x0, waiting for transfers between devices: 71.2 us -> none  [per_device(): total = lax.psum(mine, 'tp')]
    reduce_scatter x1 -> x0, waiting for transfers between devices: 57 us -> none  [per_device(): mine = lax.psum_scatter(part, 'ep', scatter_dimension=0, tiled=True)]
    dot_general x3 -> x0, matrix products: 43 us -> none  [the longest x1 27.1 us: per_device(): jnp.einsum('etf,efd->td', act, w_down, preferred_element_type=jnp.float32)]
    all_gather x1 -> x0, waiting for transfers between devices: 39.4 us -> none  [per_device(): all_rows = lax.all_gather(normed, 'ep', axis=0, tiled=True)]
    all_gather x1 -> x0, blocking collectives: 7.64 us -> none  [per_device(): all_gates = lax.all_gather(gates, 'ep', axis=0, tiled=True)]
    convert_element_type x3 -> x0, other arithmetic: 6.6 us -> none  [the longest x1 2.97 us: rms_norm(): (wide_h * lax.rsqrt(mean_sq + NORM_EPS) * norm_w.astype(jnp.float32)).ast...]
    unnamed x6 -> x2, local copies, waits for them, and re-layouts: 0.01 us -> 3.77 us
  transfers between devices with their start and end apart: 3 -> 0, of which waited for: 3 -> 0; matrix products, arithmetic and copies ran while one was open for 1% -> 0% of each run, Pallas kernels for 0% -> 0%
where the time goes in v2:
time: 98 us; the launch traced here: 97.7 us
  Pallas kernels  91.4 us (93%)
  local copies, waits for them, and re-layouts  5.88 us (6%)
    pallas_call x1, Pallas kernels, per_device(): pl.pallas_call(functools.partial(body, n_experts), out_shape=jax.ShapeDty...  91.4 us
    unnamed x2, local copies, waits for them, and re-layouts  3.77 us

profile of v2, /device:TPU:0, one launch (start us, length us, event | category | flops | bytes accessed | tf_op | source)
XLA Modules:
  0.0 97.7 jit_solution(18031483430731014727)
XLA Ops:
  0.0 1.3 %reshape.10.nw_ref = bf16[1,1536]{1,0:T(2,128)(2,1)} reshape(bf16[1536]{0:T(1024)(128)(2,1)} %param.9) | data formatting | bytes 6144 | tf_op jit(solution)/shard_map/reshape | solution.py:354
  1.3 1.1 %copy.8 = bf16[1536,40]{1,0:T(8,128)(2,1)S(1)} copy(bf16[1536,40]{0,1:T(8,128)(2,1)} %param.10) | data formatting | bytes 245760 | tf_op args[3]
  2.4 0.4 dynamic-slice_maximum_fusion
  2.8 0.8 pad.4.wr_ref
  3.7 91.4 %moe_layer.1 = bf16[512,1536]{1,0:T(8,128)(2,1)} custom-call(s32[4,8,128]{2,1,0:T(8,128)} %bitcast.5, bf16[512,1536]{1,0:T(8,128)(2,1)} %h_ref.1, bf16[1,1536]{1,0:T(2,128)(2,1)} %reshape.10.nw_ref, bf16[1536,128]{1,0:T(8,128)(2,1)} %pad.4.wr_ref, bf16[10,1536,128]{2,1,0:T(8,128)(2,1)} %wg_hbm.1, bf16[10,1536,128]{2,1,0:T(8,128)(2,1)} %wu_hbm.1, ...), custom_call_target="tpu_custom_call" | custom-call | tf_op jit(solution)/shard_map/moe_layer/pallas_call | solution.py:346
  95.1 2.7 %copy.11 = bf16[512,1536]{1,0:T(8,128)(2,1)} copy(bf16[512,1536]{1,0:T(8,128)(2,1)} %moe_layer.1) | data formatting | bytes 3145728

commit v3 on v2

v3 whole, which is shorter than its diff:
```python
import jax
import jax.numpy as jnp
from jax import lax
from jax.experimental import pallas as pl
from jax.experimental.pallas import tpu as pltpu
from jax.sharding import PartitionSpec as P

NORM_EPS = 1e-6
MESH = pl.DeviceIdType.MESH
OWN_SLOT = (0, 1, 2, 4)
FAR_SLOT = (3, 5, 6, 7)
N_SUB = 4
UNITS = ((0, 0, 32), (0, 32, 32), (1, 0, 64), (2, 0, 64), (3, 0, 64))
COLS = 512
PIECE = 16


def body(ids_hbm, h_hbm, nw_hbm, wrt_hbm, wg_hbm, wu_hbm, wd_hbm, out_ref,
         ids_ref, nw_ref, wrt_ref, h_ref, wr, v, wgu, wd, act, keep, dsend, drecv, sbuf, rbuf, tbuf, abuf, ubuf, ids_all, ids_slot,
         h_sem, w_sem, ids_s, ids_r, d1_s, d1_r, dy_s, dy_r, dz_s, dz_r, dd_s, dd_r, pd_s, pd_r,
         sy_s, sy_r, ra_s, ra_r, rb_s, rb_r, rc_s, rc_r):
    tok, dim = h_ref.shape
    n_experts = wrt_ref.shape[0]
    local_exp, _, width = wg_hbm.shape
    sub = tok // N_SUB
    half = sub // 2
    n_piece = tok // PIECE
    per_sub = sub // PIECE
    ep = lax.axis_index("ep")
    z = lax.axis_index("tp")
    core, y = ep % 2, ep // 2
    ep_pair = 2 * y + 1 - core
    ep_far = 2 * (1 - y) + core
    ep_diag = 2 * (1 - y) + 1 - core
    side = z % 2
    z_pair = z + 1 - 2 * side
    z_mirror = 3 - z
    inner = jnp.logical_or(z == 1, z == 2)
    outer = jnp.logical_or(z == 0, z == 3)

    def remote(src, dst, ssem, rsem, **where):
        return pltpu.make_async_remote_copy(src_ref=src, dst_ref=dst, send_sem=ssem, recv_sem=rsem, device_id=where, device_id_type=MESH)

    def weight_copies():
        copies = []
        for e in range(local_exp):
            copies.append(pltpu.make_async_copy(wg_hbm.at[e], wgu.at[e, :, pl.ds(0, width)], w_sem.at[2 * e]))
            copies.append(pltpu.make_async_copy(wu_hbm.at[e], wgu.at[e, :, pl.ds(width, width)], w_sem.at[2 * e + 1]))
        copies.append(pltpu.make_async_copy(wd_hbm, wd, w_sem.at[2 * local_exp]))
        return copies

    def h_copy(s):
        rows = pl.ds(s * sub, sub)
        return pltpu.make_async_copy(h_hbm.at[rows], h_ref.at[rows], h_sem.at[s])

    small = [pltpu.make_async_copy(src, dst, h_sem.at[N_SUB + k]) for k, (src, dst) in enumerate(((nw_hbm, nw_ref), (ids_hbm, ids_ref), (wrt_hbm, wrt_ref)))]
    h_copy(0).start()
    for copy in small:
        copy.start()
    for s in range(1, N_SUB):
        h_copy(s).start()
    barrier = pltpu.get_barrier_semaphore()
    for where in ({"ep": ep_pair}, {"ep": ep_far}, {"ep": ep_diag}, {"tp": z_pair}, {"tp": z_mirror}):
        pl.semaphore_signal(barrier, inc=1, device_id=where, device_id_type=MESH)
    weights = weight_copies()
    for copy in weights:
        copy.start()

    small[0].wait()
    scale = nw_ref[...].astype(jnp.float32).reshape(1, dim)

    def norm_rows(s):
        slot = OWN_SLOT[s]

        h_copy(s).wait()

        def group(i, carry):
            r = pl.multiple_of(i * 16, 16)
            x = h_ref[pl.ds(s * sub + r, 16), :].astype(jnp.float32)
            ms = jnp.mean(x * x, axis=-1, keepdims=True)
            v[slot, pl.ds(r, 16), :] = (x * lax.rsqrt(ms + NORM_EPS) * scale).astype(jnp.bfloat16)
            return carry

        lax.fori_loop(0, sub // 16, group, 0, unroll=4)

    def unit_rows(u, which, base=0):
        _, first, rows = UNITS[u]
        return pl.ds(pl.multiple_of(base + which * half + first, 16), rows)

    def ids_copy(k):
        ep_to = (ep_pair, ep_far, ep_diag)[k]
        return remote(ids_ref, ids_all.at[k], ids_s.at[k], ids_r.at[k], ep=ep_to)

    def d1(s):
        slot = OWN_SLOT[s]
        return remote(v.at[slot, pl.ds(0, sub)], v.at[slot, pl.ds(sub, sub)], d1_s.at[s], d1_r.at[s], ep=ep_pair)

    def dy(u):
        s, rows = UNITS[u][0], unit_rows(u, side)
        return remote(v.at[OWN_SLOT[s], rows], v.at[FAR_SLOT[s], rows], dy_s.at[u], dy_r.at[u], ep=ep_far)

    def dz(u, which):
        s, rows = UNITS[u][0], unit_rows(u, which)
        return remote(v.at[FAR_SLOT[s], rows], v.at[FAR_SLOT[s], rows], dz_s.at[u], dz_r.at[u], tp=z_pair)

    def dd(u, k):
        s, which = UNITS[u][0], side if k == 0 else 1 - side
        return remote(v.at[FAR_SLOT[s], unit_rows(u, which)], v.at[FAR_SLOT[s], unit_rows(u, which, sub)], dd_s.at[2 * u + k], dd_r.at[2 * u + k], ep=ep_pair)

    def pd(slot, n):
        cols = pl.ds(n * COLS, COLS)
        k = slot * (dim // COLS) + n
        return remote(dsend.at[slot, :, cols], drecv.at[slot, :, cols], pd_s.at[k], pd_r.at[k], ep=ep_pair)

    def pair_part(slot):
        for n in range(dim // COLS):
            pd(slot, n).wait_recv()

    def piece_rows(p):
        return pl.ds(pl.multiple_of(p * PIECE, PIECE), PIECE)

    def sy(p):
        return remote(sbuf.at[piece_rows(p)], rbuf.at[piece_rows(p)], sy_s.at[p], sy_r.at[p], ep=ep_far)

    def ra(p):
        return remote(tbuf.at[piece_rows(p)], abuf.at[piece_rows(p)], ra_s.at[p], ra_r.at[p], tp=z_pair)

    def rb(p):
        return remote(tbuf.at[piece_rows(p)], ubuf.at[piece_rows(p)], rb_s.at[p], rb_r.at[p], tp=z_mirror)

    def rc(p):
        return remote(out_ref.at[piece_rows(p)], out_ref.at[piece_rows(p)], rc_s.at[p], rc_r.at[p], tp=z_pair)

    norm_rows(0)
    pl.semaphore_wait(barrier, 5)
    for s in range(N_SUB):
        if s:
            norm_rows(s)
        for u, unit in enumerate(UNITS):
            if unit[0] == s:
                dy(u).start()
        d1(s).start()
        if s == 0:
            small[1].wait()
            for k in range(3):
                ids_copy(k).start()

    def far_in(u):
        dy(u).wait_recv()
        dz(u, side).start()
        dd(u, 0).start()

    def far_pair_in(u):
        dz(u, 1 - side).wait_recv()
        dd(u, 1).start()

    def far_ready(s):
        for u, unit in enumerate(UNITS):
            if unit[0] == s:
                dd(u, 0).wait_recv()
                dd(u, 1).wait_recv()

    def ids_own():
        ids_copy(0).wait_recv()
        for s in range(N_SUB):
            ids_slot[OWN_SLOT[s], 0] = ids_ref[s]
            ids_slot[OWN_SLOT[s], 1] = ids_all[0, s]

    def ids_far():
        ids_copy(1).wait_recv()
        ids_copy(2).wait_recv()
        for s in range(N_SUB):
            ids_slot[FAR_SLOT[s], 0] = ids_all[1, s]
            ids_slot[FAR_SLOT[s], 1] = ids_all[2, s]

    def far_sum(s):
        slot = FAR_SLOT[s]
        pair_part(slot)

        def one(i, carry):
            r = pl.multiple_of(i * PIECE, PIECE)
            total = keep[slot, pl.ds(r, PIECE), :] + drecv[slot, pl.ds(r, PIECE), :].astype(jnp.float32)
            sbuf[pl.ds(s * sub + r, PIECE), :] = total.astype(jnp.bfloat16)
            sy(s * per_sub + i).start()
            return carry

        lax.fori_loop(0, per_sub, one, 0)

    small[2].wait()
    wide = jnp.concatenate([wrt_ref[...].astype(jnp.float32), jnp.zeros((128 - n_experts, dim), jnp.float32)], axis=0)
    wr[...] = wide.T.astype(jnp.bfloat16)

    def total_of(p):
        s = p // per_sub
        slot = s + s // 3
        at = p - s * per_sub

        @pl.when(at == 0)
        def _():
            pair_part(slot)

        sy(p).wait_recv()
        rows = pl.ds(pl.multiple_of(at * PIECE, PIECE), PIECE)
        return keep[slot, rows, :] + drecv[slot, rows, :].astype(jnp.float32) + rbuf[piece_rows(p), :].astype(jnp.float32)

    def send_out(p):
        tbuf[piece_rows(p), :] = total_of(p).astype(jnp.bfloat16)
        ra(p).start()

    def join_in(p):
        total = total_of(p)
        ra(p).wait_recv()
        tbuf[piece_rows(p), :] = (total + abuf[piece_rows(p), :].astype(jnp.float32)).astype(jnp.bfloat16)
        rb(p).start()

    def finish(p):
        rb(p).wait_recv()
        rows = piece_rows(p)
        total = tbuf[rows, :].astype(jnp.float32) + ubuf[rows, :].astype(jnp.float32)
        out_ref[rows, :] = (h_ref[rows, :].astype(jnp.float32) + total).astype(jnp.bfloat16)
        rc(p).start()

    def pieces(rows_32):
        return [q for p in rows_32 for q in (2 * p, 2 * p + 1)]

    def line(out=(), joined=(), done=()):
        @pl.when(outer)
        def _():
            for p in pieces(out):
                send_out(p)

        @pl.when(inner)
        def _():
            for p in pieces(joined):
                join_in(p)
            for p in pieces(done):
                finish(p)

    def weights_in(which):
        for copy in which:
            copy.wait()

    pre = {0: [lambda: d1(0).wait_recv(), ids_own, lambda: weights_in(weights[:-1])],
           1: [lambda: far_in(0), lambda: d1(1).wait_recv()],
           2: [lambda: d1(2).wait_recv()],
           3: [ids_far, lambda: far_ready(0)],
           4: [lambda: far_sum(0), lambda: far_in(4), lambda: far_pair_in(2), lambda: d1(3).wait_recv()],
           5: [lambda: line((0,)), lambda: far_pair_in(3), lambda: far_ready(1)],
           6: [lambda: line((2,), (0,)), lambda: far_sum(1), lambda: far_pair_in(4), lambda: far_ready(2)],
           7: [lambda: line((4,), (2,)), lambda: far_ready(3)]}
    mid = {0: [lambda: weights_in(weights[-1:])],
           1: [lambda: far_in(1)],
           2: [lambda: far_in(2), lambda: far_pair_in(0), lambda: far_pair_in(1)],
           3: [lambda: far_in(3)],
           5: [lambda: line((1,))],
           6: [lambda: line((3,), (1,), (0,))],
           7: [lambda: far_sum(2), lambda: line((5,), (3,), (1,))]}

    def run(tasks, step):
        for k, fns in tasks.items():
            @pl.when(step == k)
            def _(fns=fns):
                for fn in fns:
                    fn()

    def chosen_of(tile):
        expert = lax.broadcasted_iota(jnp.int32, (n_experts, sub), 0)
        hit = jnp.zeros((n_experts, sub), jnp.float32)
        for j in range(tile.shape[0]):
            hit = jnp.where(tile[j:j + 1, :] == expert, 1.0, hit)
        return jnp.concatenate([hit, jnp.zeros((128 - n_experts, sub), jnp.float32)], axis=0).T

    @pl.loop(0, 2 * N_SUB)
    def _(step):
        run(pre, step)
        x = v.at[step]
        logits = jnp.dot(x[...], wr[...], preferred_element_type=jnp.float32)
        lane = lax.broadcasted_iota(jnp.int32, logits.shape, 1)
        logits = jnp.where(lane < n_experts, logits, -jnp.inf)
        raised = jnp.exp(logits - jnp.max(logits, axis=-1, keepdims=True))
        prob = raised / jnp.sum(raised, axis=-1, keepdims=True)
        chosen = jnp.concatenate([chosen_of(ids_slot[step, 0]), chosen_of(ids_slot[step, 1])], axis=0)
        gates = pltpu.roll(prob * chosen, (128 - ep * local_exp) % 128, axis=1)
        for e in range(local_exp):
            gu = jnp.dot(x[...], wgu[e], preferred_element_type=jnp.float32)
            a = (jax.nn.silu(gu[:, :width]) * gu[:, width:]).astype(jnp.bfloat16).astype(jnp.float32)
            act[:, e * width:(e + 1) * width] = (a * gates[:, e:e + 1]).astype(jnp.bfloat16)
        run(mid, step)
        for n in range(dim // COLS):
            part = jnp.dot(act[...], wd[:, n * COLS:(n + 1) * COLS], preferred_element_type=jnp.float32)
            keep[step, :, n * COLS:(n + 1) * COLS] = part[:sub]
            dsend[step, :, n * COLS:(n + 1) * COLS] = part[sub:].astype(jnp.bfloat16)
        for n in range(dim // COLS):
            pd(step, n).start()

    @pl.when(outer)
    def _():
        @pl.loop(12, n_piece)
        def _(p):
            @pl.when(p == 16)
            def _():
                far_sum(3)

            send_out(p)

        @pl.loop(0, n_piece)
        def _(p):
            rc(p).wait_recv()

    @pl.when(inner)
    def _():
        finish(4)

        @pl.loop(8, n_piece)
        def _(p):
            @pl.when(p == 10)
            def _():
                far_sum(3)

            join_in(p)
            finish(p - 3)

        finish(n_piece - 3)
        finish(n_piece - 2)
        finish(n_piece - 1)

    for k in range(3):
        ids_copy(k).wait_send()
    for s in range(N_SUB):
        d1(s).wait_send()
    for u in range(len(UNITS)):
        dy(u).wait_send()
        dz(u, side).wait_send()
        dd(u, 0).wait_send()
        dd(u, 1).wait_send()

    @pl.loop(0, 2 * N_SUB)
    def _(slot):
        for n in range(dim // COLS):
            pd(slot, n).wait_send()

    @pl.loop(0, n_piece)
    def _(p):
        sy(p).wait_send()

        @pl.when(outer)
        def _():
            ra(p).wait_send()

        @pl.when(inner)
        def _():
            rb(p).wait_send()
            rc(p).wait_send()


def solution(mesh):
    def per_device(hidden, expert_ids, norm_w, router_w, w_gate, w_up, w_down):
        tok, dim = hidden.shape
        top_k = expert_ids.shape[1]
        local_exp, _, width = w_gate.shape
        sub = tok // N_SUB
        n_piece = tok // PIECE
        ids_t = expert_ids.reshape(N_SUB, sub, top_k).transpose(0, 2, 1)
        bf, f32 = jnp.bfloat16, jnp.float32
        vmem = pl.BlockSpec(memory_space=pltpu.VMEM)
        hbm = pl.BlockSpec(memory_space=pltpu.HBM)
        dma = pltpu.SemaphoreType.DMA
        scratch = [
            pltpu.VMEM((N_SUB, top_k, sub), jnp.int32),
            pltpu.VMEM((dim,), bf),
            pltpu.VMEM((router_w.shape[1], dim), bf),
            pltpu.VMEM((tok, dim), bf),
            pltpu.VMEM((dim, 128), bf),
            pltpu.VMEM((2 * N_SUB, 2 * sub, dim), bf),
            pltpu.VMEM((local_exp, dim, 2 * width), bf),
            pltpu.VMEM((local_exp * width, dim), bf),
            pltpu.VMEM((2 * sub, local_exp * width), bf),
            pltpu.VMEM((2 * N_SUB, sub, dim), f32),
            pltpu.VMEM((2 * N_SUB, sub, dim), bf),
            pltpu.VMEM((2 * N_SUB, sub, dim), bf),
            pltpu.VMEM((tok, dim), bf),
            pltpu.VMEM((tok, dim), bf),
            pltpu.VMEM((tok, dim), bf),
            pltpu.VMEM((tok, dim), bf),
            pltpu.VMEM((tok, dim), bf),
            pltpu.VMEM((3, N_SUB, top_k, sub), jnp.int32),
            pltpu.VMEM((2 * N_SUB, 2, top_k, sub), jnp.int32),
            dma((N_SUB + 3,)),
            dma((2 * local_exp + 1,)),
            dma((3,)), dma((3,)),
            dma((N_SUB,)), dma((N_SUB,)),
            dma((len(UNITS),)), dma((len(UNITS),)),
            dma((len(UNITS),)), dma((len(UNITS),)),
            dma((2 * len(UNITS),)), dma((2 * len(UNITS),)),
            dma((2 * N_SUB * dim // COLS,)), dma((2 * N_SUB * dim // COLS,)),
            dma((n_piece,)), dma((n_piece,)),
            dma((n_piece,)), dma((n_piece,)),
            dma((n_piece,)), dma((n_piece,)),
            dma((n_piece,)), dma((n_piece,)),
        ]
        return pl.pallas_call(
            body,
            out_shape=jax.ShapeDtypeStruct((tok, dim), bf),
            in_specs=[hbm] * 7,
            out_specs=vmem,
            scratch_shapes=scratch,
            compiler_params=pltpu.CompilerParams(collective_id=0, has_side_effects=True, vmem_limit_bytes=53_000_000),
            name="moe_layer",
        )(*[pltpu.with_memory_space_constraint(x, pltpu.HBM) for x in (ids_t, hidden, norm_w, router_w.T, w_gate, w_up, w_down.reshape(local_exp * width, dim))])

    token_spec = P(("dp", "ep"), None)
    return jax.shard_map(per_device, mesh=mesh, in_specs=(token_spec, token_spec, P(None), P(None, None), P("ep", None, "tp"), P("ep", None, "tp"), P("ep", "tp", None)), out_specs=token_spec, check_vma=False)
```

time: 98 us -> 79.3 us (0.81)
  Pallas kernels: 91.4 us -> 78 us
  local copies, waits for them, and re-layouts: 5.88 us -> 1.15 us
    pallas_call x1, Pallas kernels: 91.4 us -> 78 us  [per_device(): pl.pallas_call(body, out_shape=jax.ShapeDtypeStruct((tok, dim), bf), in_s...]
    unnamed x2 -> x1, local copies, waits for them, and re-layouts: 3.77 us -> 1.15 us
    reshape x1 -> x0, local copies, waits for them, and re-layouts: 1.28 us -> none  [per_device(): norm_w.reshape(1, dim)]
where the time goes in v3:
time: 79.3 us; the launch traced here: 79.1 us
  Pallas kernels  78 us (98%)
  local copies, waits for them, and re-layouts  1.15 us (1%)
    pallas_call x1, Pallas kernels, per_device(): pl.pallas_call(body, out_shape=jax.ShapeDtypeStruct((tok, dim), bf), in_s...  78 us

profile of v3, /device:TPU:0, one launch (start us, length us, event | category | flops | bytes accessed | tf_op | source)
XLA Modules:
  0.0 79.1 jit_solution(12763618785552736430)
XLA Ops:
  0.0 78.0 %moe_layer.1 = bf16[512,1536]{1,0:T(8,128)(2,1)S(1)} custom-call(s32[4,8,128]{2,1,0:T(8,128)} %bitcast.7, bf16[512,1536]{1,0:T(8,128)(2,1)} %h_hbm.1, bf16[1536]{0:T(1024)(128)(2,1)} %nw_hbm.1, bf16[40,1536]{1,0:T(8,128)(2,1)} %bitcast.6, bf16[10,1536,128]{2,1,0:T(8,128)(2,1)} %wg_hbm.1, bf16[10,1536,128]{2,1,0:T(8,128)(2,1)} %wu_hbm.1, ...), custom_call_target="tpu_custom_call" | custom-call | tf_op jit(solution)/shard_map/moe_layer/pallas_call | solution.py:401
  78.0 1.1 %copy.9 = bf16[512,1536]{1,0:T(8,128)(2,1)} copy(bf16[512,1536]{1,0:T(8,128)(2,1)S(1)} %moe_layer.1) | data formatting | bytes 3145728

commit v4 on v1

v4 whole, which is shorter than its diff:
```python
import jax
import jax.numpy as jnp
from jax import lax
from jax.experimental import pallas as pl
from jax.experimental.pallas import tpu as pltpu
from jax.sharding import PartitionSpec as P

NORM_EPS = 1e-6
MESH = pl.DeviceIdType.MESH
N_BLK = 8
PIECE = 16
COLS = 512
JOBS = (
    (("own", 0), ("own", 1)),
    (("own", 2), ("own", 3)),
    (("far", 0), ("own", 4)),
    (("far", 1), ("own", 5)),
    (("far", 2), ("far", 3)),
    (("far", 4), ("far", 5)),
    (("own", 6), ("own", 7)),
    (("far", 6), ("far", 7)),
)
PLACE = {block: (slot, k) for slot, job in enumerate(JOBS) for k, block in enumerate(job)}
WHOLE = 6
UNITS = ((0, 0, 16), (0, 16, 16)) + tuple((b, 0, 32) for b in range(1, WHOLE))


def body(ids_hbm, h_hbm, nw_hbm, wrt_hbm, wg_hbm, wu_hbm, wd_hbm, out_ref,
         ids_ref, nw_ref, wrt_ref, h_ref, wr, v, wgu, wd, act, keep, dsend, drecv, sbuf, rbuf, tbuf, abuf, ubuf, ids_all, ids_slot,
         h_sem, w_sem, ids_s, ids_r, d1_s, d1_r, dy_s, dy_r, dz_s, dz_r, dyw_s, dyw_r, dzw_s, dzw_r, dd_s, dd_r, pd_s, pd_r,
         sy_s, sy_r, rac_s, rac_r, rb_s, rb_r):
    tok, dim = h_ref.shape
    n_experts = wrt_ref.shape[0]
    local_exp, _, width = wg_hbm.shape
    blk = tok // N_BLK
    half = blk // 2
    mine = 2 * blk
    n_job = len(JOBS)
    n_piece = tok // PIECE
    per_blk = blk // PIECE
    ep = lax.axis_index("ep")
    z = lax.axis_index("tp")
    core, y = ep % 2, ep // 2
    ep_pair = 2 * y + 1 - core
    ep_far = 2 * (1 - y) + core
    ep_diag = 2 * (1 - y) + 1 - core
    side = z % 2
    z_pair = z + 1 - 2 * side
    z_mirror = 3 - z
    inner = jnp.logical_or(z == 1, z == 2)
    outer = jnp.logical_or(z == 0, z == 3)

    def remote(src, dst, ssem, rsem, **where):
        return pltpu.make_async_remote_copy(src_ref=src, dst_ref=dst, send_sem=ssem, recv_sem=rsem, device_id=where, device_id_type=MESH)

    def weight_copies():
        copies = []
        for e in range(local_exp):
            copies.append(pltpu.make_async_copy(wg_hbm.at[e], wgu.at[e, :, pl.ds(0, width)], w_sem.at[0]))
            copies.append(pltpu.make_async_copy(wu_hbm.at[e], wgu.at[e, :, pl.ds(width, width)], w_sem.at[0]))
        copies.append(pltpu.make_async_copy(wd_hbm, wd, w_sem.at[1]))
        return copies

    def h_copy(k):
        rows = pl.ds(k * mine, mine)
        return pltpu.make_async_copy(h_hbm.at[rows], h_ref.at[rows], h_sem.at[k])

    n_h = tok // mine
    small = [pltpu.make_async_copy(src, dst, h_sem.at[n_h + k]) for k, (src, dst) in enumerate(((nw_hbm, nw_ref), (ids_hbm, ids_ref), (wrt_hbm, wrt_ref)))]
    h_copy(0).start()
    for copy in small:
        copy.start()
    for k in range(1, n_h):
        h_copy(k).start()
    barrier = pltpu.get_barrier_semaphore()
    for where in ({"ep": ep_pair}, {"ep": ep_far}, {"ep": ep_diag}, {"tp": z_pair}, {"tp": z_mirror}):
        pl.semaphore_signal(barrier, inc=1, device_id=where, device_id_type=MESH)
    for copy in weight_copies():
        copy.start()

    small[0].wait()
    scale = nw_ref[...].astype(jnp.float32).reshape(1, dim)

    def norm_block(b):
        slot, k = PLACE["own", b]
        if b % 2 == 0:
            h_copy(b // 2).wait()

        def group(i, carry):
            r = pl.multiple_of(i * 16, 16)
            x = h_ref[pl.ds(b * blk + r, 16), :].astype(jnp.float32)
            ms = jnp.mean(x * x, axis=-1, keepdims=True)
            v[slot, pl.ds(k * blk + r, 16), :] = (x * lax.rsqrt(ms + NORM_EPS) * scale).astype(jnp.bfloat16)
            return carry

        lax.fori_loop(0, blk // 16, group, 0, unroll=True)

    def unit(kind, u, which, base=0):
        b, first, rows = UNITS[u]
        slot, k = PLACE[kind, b]
        return v.at[slot, pl.ds(pl.multiple_of(base + k * blk + which * half + first, 16), rows)]

    def block(kind, b, base=0):
        slot, k = PLACE[kind, b]
        return v.at[slot, pl.ds(base + k * blk, blk)]

    def ids_copy(k):
        ep_to = (ep_pair, ep_far, ep_diag)[k]
        return remote(ids_ref, ids_all.at[k], ids_s, ids_r.at[k], ep=ep_to)

    def d1(b):
        return remote(block("own", b), block("own", b, mine), d1_s, d1_r.at[PLACE["own", b][0]], ep=ep_pair)

    def dy(u):
        return remote(unit("own", u, side), unit("far", u, side), dy_s, dy_r.at[u], ep=ep_far)

    def dz(u, which):
        return remote(unit("far", u, which), unit("far", u, which), dz_s, dz_r.at[u], tp=z_pair)

    def dd(u, which):
        return remote(unit("far", u, which), unit("far", u, which, mine), dd_s, dd_r.at[UNITS[u][0]], ep=ep_pair)

    def dy_whole(b):
        return remote(block("own", b), block("far", b), dyw_s, dyw_r.at[b - WHOLE], ep=ep_far)

    def dz_whole(b):
        return remote(block("far", b), block("far", b), dzw_s, dzw_r.at[b - WHOLE], tp=z_pair)

    def dd_whole(b):
        return remote(block("far", b), block("far", b, mine), dd_s, dd_r.at[b], ep=ep_pair)

    def pd(slot, n):
        cols = pl.ds(n * COLS, COLS)
        return remote(dsend.at[slot, :, cols], drecv.at[slot, :, cols], pd_s, pd_r.at[slot], ep=ep_pair)

    def piece_rows(p):
        return pl.ds(pl.multiple_of(p * PIECE, PIECE), PIECE)

    def sy(p):
        return remote(sbuf.at[piece_rows(p)], rbuf.at[piece_rows(p)], sy_s, sy_r.at[p], ep=ep_far)

    def ra(p):
        return remote(tbuf.at[piece_rows(p)], abuf.at[piece_rows(p)], rac_s, rac_r.at[p], tp=z_pair)

    def rb(p):
        return remote(tbuf.at[piece_rows(p)], ubuf.at[piece_rows(p)], rb_s, rb_r.at[p], tp=z_mirror)

    def rc(p):
        return remote(out_ref.at[piece_rows(p)], out_ref.at[piece_rows(p)], rac_s, rac_r.at[p], tp=z_pair)

    for b in range(N_BLK):
        norm_block(b)
        if b == 0:
            pl.semaphore_wait(barrier, 5)
        for u, (of, _, _) in enumerate(UNITS):
            if of == b:
                dy(u).start()
        if b >= WHOLE:
            @pl.when(inner)
            def _(b=b):
                dy_whole(b).start()
        d1(b).start()
        if b == 0:
            small[1].wait()
            for k in range(3):
                ids_copy(k).start()

    def own_in(slot):
        of_job = [b for kind, b in JOBS[slot] if kind == "own"]
        rows = v.at[slot, pl.ds(mine + PLACE["own", of_job[0]][1] * blk, len(of_job) * blk)]
        remote(rows, rows, d1_s, d1_r.at[slot], ep=ep_pair).wait_recv()

    def far_in(u):
        dy(u).wait_recv()
        dz(u, side).start()
        dd(u, side).start()

    def far_pair_in(u):
        dz(u, 1 - side).wait_recv()
        dd(u, 1 - side).start()

    def whole_in(b):
        @pl.when(inner)
        def _():
            dy_whole(b).wait_recv()
            dz_whole(b).start()
            dd_whole(b).start()

    def whole_pair_in(b):
        @pl.when(outer)
        def _():
            dz_whole(b).wait_recv()
            dd_whole(b).start()

    def far_ready(*blocks):
        for b in blocks:
            remote(block("far", b), block("far", b, mine), dd_s, dd_r.at[b], ep=ep_pair).wait_recv()

    def ids_own():
        ids_copy(0).wait_recv()
        for b in range(N_BLK):
            slot, k = PLACE["own", b]
            lanes, at = slice(b % 2 * blk, (b % 2 + 1) * blk), slice(k * blk, (k + 1) * blk)
            ids_slot[slot, 0, :, at] = ids_ref[b // 2, :, lanes]
            ids_slot[slot, 1, :, at] = ids_all[0, b // 2, :, lanes]

    def ids_far():
        ids_copy(1).wait_recv()
        ids_copy(2).wait_recv()
        for b in range(N_BLK):
            slot, k = PLACE["far", b]
            lanes, at = slice(b % 2 * blk, (b % 2 + 1) * blk), slice(k * blk, (k + 1) * blk)
            ids_slot[slot, 0, :, at] = ids_all[1, b // 2, :, lanes]
            ids_slot[slot, 1, :, at] = ids_all[2, b // 2, :, lanes]

    def pair_part(slot):
        remote(dsend.at[slot], drecv.at[slot], pd_s, pd_r.at[slot], ep=ep_pair).wait_recv()

    def far_sum(b):
        slot, k = PLACE["far", b]

        def one(i, carry):
            rows = pl.ds(pl.multiple_of(k * blk + i * PIECE, PIECE), PIECE)
            total = keep[slot, rows, :] + drecv[slot, rows, :].astype(jnp.float32)
            sbuf[piece_rows(b * per_blk + i), :] = total.astype(jnp.bfloat16)
            sy(b * per_blk + i).start()
            return carry

        lax.fori_loop(0, per_blk, one, 0)

    small[2].wait()
    wide = jnp.concatenate([wrt_ref[...].astype(jnp.float32), jnp.zeros((128 - n_experts, dim), jnp.float32)], axis=0)
    wr[...] = wide.T.astype(jnp.bfloat16)

    def total_of(b, i):
        slot, k = PLACE["own", b]
        p = b * per_blk + i
        sy(p).wait_recv()
        rows = pl.ds(pl.multiple_of(k * blk + i * PIECE, PIECE), PIECE)
        return keep[slot, rows, :] + drecv[slot, rows, :].astype(jnp.float32) + rbuf[piece_rows(p), :].astype(jnp.float32)

    def send_out(b, i):
        p = b * per_blk + i
        tbuf[piece_rows(p), :] = total_of(b, i).astype(jnp.bfloat16)
        ra(p).start()

    def join_in(b, i):
        p = b * per_blk + i
        total = total_of(b, i)
        ra(p).wait_recv()
        tbuf[piece_rows(p), :] = (total + abuf[piece_rows(p), :].astype(jnp.float32)).astype(jnp.bfloat16)
        rb(p).start()

    def finish(p):
        rb(p).wait_recv()
        rows = piece_rows(p)
        total = tbuf[rows, :].astype(jnp.float32) + ubuf[rows, :].astype(jnp.float32)
        out_ref[rows, :] = (h_ref[rows, :].astype(jnp.float32) + total).astype(jnp.bfloat16)
        rc(p).start()

    def line(out=(), joined=(), done=()):
        @pl.when(outer)
        def _():
            for p in out:
                send_out(*divmod(p, per_blk))

        @pl.when(inner)
        def _():
            for p in joined:
                join_in(*divmod(p, per_blk))
            for p in done:
                finish(p)

    def weights_in(ref, k):
        pltpu.make_async_copy(ref, ref, w_sem.at[k]).wait()

    def each(fn, *args):
        return lambda: fn(*args)

    pre = {0: [each(own_in, 0), ids_own, each(weights_in, wgu, 0)],
           1: [each(far_in, 1), each(own_in, 1)],
           2: [ids_far, each(own_in, 2), each(far_in, 3), each(far_ready, 0)],
           3: [each(far_in, 5), each(pair_part, 2), each(far_sum, 0), each(far_pair_in, 3),
               each(own_in, 3), each(far_ready, 1), each(pair_part, 0), each(pair_part, 1)],
           4: [each(whole_in, 6), each(far_pair_in, 5), each(line, (0,)), each(far_ready, 2, 3)],
           5: [each(line, (), (0,)), each(whole_in, 7), each(far_ready, 4, 5)],
           6: [each(line, (6,), (3,), (0,)), each(whole_pair_in, 6), each(own_in, 6)],
           7: [each(line, (10, 11), (6, 7), (3,)), each(far_ready, 6, 7)]}
    early = {2: [each(far_in, 4)],
             3: [each(far_in, 6), each(far_pair_in, 4)],
             4: [each(pair_part, 3), each(far_sum, 1), each(line, (1, 2))],
             5: [each(pair_part, 4), each(far_sum, 2), each(far_sum, 3), each(line, (4,), (1,))],
             6: [each(pair_part, 5), each(far_sum, 4), each(far_sum, 5), each(line, (7, 8), (4,), (1,))],
             7: [each(pair_part, 6), each(line, (12,), (8,), (4,))]}
    mid = {0: [each(weights_in, wd, 1), each(far_in, 0)],
           1: [each(far_in, 2), each(far_pair_in, 0), each(far_pair_in, 1)],
           2: [each(far_pair_in, 2)],
           4: [each(line, (3,)), each(far_pair_in, 6)],
           5: [each(line, (5,), (2,))],
           6: [each(line, (9,), (5,), (2,)), each(whole_pair_in, 7)],
           7: [each(line, (13, 14), (9, 10), (5, 6))]}
    out_from, join_from, lag = 15, 11, 4

    def run(tasks, step):
        for k, fns in tasks.items():
            @pl.when(step == k)
            def _(fns=fns):
                for fn in fns:
                    fn()

    def chosen_of(tile):
        expert = lax.broadcasted_iota(jnp.int32, (n_experts, mine), 0)
        hit = jnp.zeros((n_experts, mine), jnp.float32)
        for j in range(tile.shape[0]):
            hit = jnp.where(tile[j:j + 1, :] == expert, 1.0, hit)
        return jnp.concatenate([hit, jnp.zeros((128 - n_experts, mine), jnp.float32)], axis=0).T

    @pl.loop(0, n_job)
    def _(step):
        run(pre, step)
        x = v.at[step]
        logits = jnp.dot(x[...], wr[...], preferred_element_type=jnp.float32)
        lane = lax.broadcasted_iota(jnp.int32, logits.shape, 1)
        logits = jnp.where(lane < n_experts, logits, -jnp.inf)
        raised = jnp.exp(logits - jnp.max(logits, axis=-1, keepdims=True))
        prob = raised / jnp.sum(raised, axis=-1, keepdims=True)
        chosen = jnp.concatenate([chosen_of(ids_slot[step, 0]), chosen_of(ids_slot[step, 1])], axis=0)
        gates = pltpu.roll(prob * chosen, (128 - ep * local_exp) % 128, axis=1)
        for e in range(local_exp):
            gu = jnp.dot(x[...], wgu[e], preferred_element_type=jnp.float32)
            if e == local_exp // 2:
                run(early, step)
            a = (jax.nn.silu(gu[:, :width]) * gu[:, width:]).astype(jnp.bfloat16).astype(jnp.float32)
            act[:, e * width:(e + 1) * width] = (a * gates[:, e:e + 1]).astype(jnp.bfloat16)
        run(mid, step)
        for n in range(dim // COLS):
            part = jnp.dot(act[...], wd[:, n * COLS:(n + 1) * COLS], preferred_element_type=jnp.float32)
            keep[step, :, n * COLS:(n + 1) * COLS] = part[:mine]
            dsend[step, :, n * COLS:(n + 1) * COLS] = part[mine:].astype(jnp.bfloat16)
        for n in range(dim // COLS):
            pd(step, n).start()

    @pl.when(outer)
    def _():
        for b in range(out_from // per_blk, N_BLK):
            if b == 4:
                pair_part(7)
                far_sum(6)
                far_sum(7)

            @pl.loop(max(out_from - b * per_blk, 0), per_blk)
            def _(i, b=b):
                send_out(b, i)

        @pl.loop(0, n_piece)
        def _(p):
            rc(p).wait_recv()

    @pl.when(inner)
    def _():
        for b in range(join_from // per_blk, N_BLK):
            if b == 4:
                pair_part(7)
                far_sum(6)
                far_sum(7)

            @pl.loop(max(join_from - b * per_blk, 0), per_blk)
            def _(i, b=b):
                join_in(b, i)
                finish(b * per_blk + i - lag)

        for p in range(n_piece - lag, n_piece):
            finish(p)

    remote(ids_all, ids_all, ids_s, ids_r.at[0], ep=ep_pair).wait_send()
    two, shared, whole = v.at[pl.ds(0, 2)], v.at[0, pl.ds(0, WHOLE * half)], v.at[0, pl.ds(0, (N_BLK - WHOLE) * blk)]
    remote(two, two, d1_s, d1_r.at[0], ep=ep_pair).wait_send()
    remote(shared, shared, dy_s, dy_r.at[0], ep=ep_far).wait_send()
    remote(shared, shared, dz_s, dz_r.at[0], tp=z_pair).wait_send()
    remote(two, two, dd_s, dd_r.at[0], ep=ep_pair).wait_send()
    remote(dsend, drecv, pd_s, pd_r.at[0], ep=ep_pair).wait_send()
    remote(sbuf, rbuf, sy_s, sy_r.at[0], ep=ep_far).wait_send()

    @pl.when(outer)
    def _():
        remote(tbuf, abuf, rac_s, rac_r.at[0], tp=z_pair).wait_send()

    @pl.when(inner)
    def _():
        remote(whole, whole, dyw_s, dyw_r.at[0], ep=ep_far).wait_send()
        remote(whole, whole, dzw_s, dzw_r.at[0], tp=z_pair).wait_send()
        remote(tbuf, ubuf, rb_s, rb_r.at[0], tp=z_mirror).wait_send()
        remote(out_ref, out_ref, rac_s, rac_r.at[0], tp=z_pair).wait_send()


def solution(mesh):
    def per_device(hidden, expert_ids, norm_w, router_w, w_gate, w_up, w_down):
        tok, dim = hidden.shape
        top_k = expert_ids.shape[1]
        local_exp, _, width = w_gate.shape
        blk = tok // N_BLK
        n_job = len(JOBS)
        n_piece = tok // PIECE
        ids_t = expert_ids.reshape(N_BLK // 2, 2 * blk, top_k).transpose(0, 2, 1)
        bf, f32 = jnp.bfloat16, jnp.float32
        dma = pltpu.SemaphoreType.DMA
        scratch = [
            pltpu.VMEM((N_BLK // 2, top_k, 2 * blk), jnp.int32),
            pltpu.VMEM((dim,), bf),
            pltpu.VMEM((router_w.shape[1], dim), bf),
            pltpu.VMEM((tok, dim), bf),
            pltpu.VMEM((dim, 128), bf),
            pltpu.VMEM((n_job, 4 * blk, dim), bf),
            pltpu.VMEM((local_exp, dim, 2 * width), bf),
            pltpu.VMEM((local_exp * width, dim), bf),
            pltpu.VMEM((4 * blk, local_exp * width), bf),
            pltpu.VMEM((n_job, 2 * blk, dim), f32),
            pltpu.VMEM((n_job, 2 * blk, dim), bf),
            pltpu.VMEM((n_job, 2 * blk, dim), bf),
            pltpu.VMEM((tok, dim), bf),
            pltpu.VMEM((tok, dim), bf),
            pltpu.VMEM((tok, dim), bf),
            pltpu.VMEM((tok, dim), bf),
            pltpu.VMEM((tok, dim), bf),
            pltpu.VMEM((3, N_BLK // 2, top_k, 2 * blk), jnp.int32),
            pltpu.VMEM((n_job, 2, top_k, 2 * blk), jnp.int32),
            dma((tok // (2 * blk) + 3,)),
            dma((2,)),
            dma, dma((3,)),
            dma, dma((n_job,)),
            dma, dma((len(UNITS),)),
            dma, dma((len(UNITS),)),
            dma, dma((N_BLK - WHOLE,)),
            dma, dma((N_BLK - WHOLE,)),
            dma, dma((N_BLK,)),
            dma, dma((n_job,)),
            dma, dma((n_piece,)),
            dma, dma((n_piece,)),
            dma, dma((n_piece,)),
        ]
        operands = (ids_t, hidden, norm_w, router_w.T, w_gate, w_up, w_down.reshape(local_exp * width, dim))
        return pl.pallas_call(
            body,
            out_shape=jax.ShapeDtypeStruct((tok, dim), bf),
            in_specs=[pl.BlockSpec(memory_space=pltpu.HBM)] * len(operands),
            out_specs=pl.BlockSpec(memory_space=pltpu.VMEM),
            scratch_shapes=scratch,
            compiler_params=pltpu.CompilerParams(collective_id=0, has_side_effects=True, vmem_limit_bytes=53_000_000),
            name="moe_layer",
        )(*[pltpu.with_memory_space_constraint(x, pltpu.HBM) for x in operands])

    token_spec = P(("dp", "ep"), None)
    return jax.shard_map(per_device, mesh=mesh, in_specs=(token_spec, token_spec, P(None), P(None, None), P("ep", None, "tp"), P("ep", None, "tp"), P("ep", "tp", None)), out_specs=token_spec, check_vma=False)
```

time: 240 us -> 74.5 us (0.31)
  waiting for transfers between devices: 168 us -> 0 us
  Pallas kernels: 0 us -> 73.2 us
  matrix products: 43 us -> 0 us
  between operations: 13.2 us -> 0.01 us
  other arithmetic: 8.61 us -> 0 us
  blocking collectives: 7.64 us -> 0 us
    pallas_call x0 -> x1, Pallas kernels: none -> 73.2 us  [per_device(): pl.pallas_call(body, out_shape=jax.ShapeDtypeStruct((tok, dim), bf), in_s...]
    psum x1 -> x0, waiting for transfers between devices: 71.2 us -> none  [per_device(): total = lax.psum(mine, 'tp')]
    reduce_scatter x1 -> x0, waiting for transfers between devices: 57 us -> none  [per_device(): mine = lax.psum_scatter(part, 'ep', scatter_dimension=0, tiled=True)]
    dot_general x3 -> x0, matrix products: 43 us -> none  [the longest x1 27.1 us: per_device(): jnp.einsum('etf,efd->td', act, w_down, preferred_element_type=jnp.float32)]
    all_gather x1 -> x0, waiting for transfers between devices: 39.4 us -> none  [per_device(): all_rows = lax.all_gather(normed, 'ep', axis=0, tiled=True)]
    all_gather x1 -> x0, blocking collectives: 7.64 us -> none  [per_device(): all_gates = lax.all_gather(gates, 'ep', axis=0, tiled=True)]
    convert_element_type x3 -> x0, other arithmetic: 6.6 us -> none  [the longest x1 2.97 us: rms_norm(): (wide_h * lax.rsqrt(mean_sq + NORM_EPS) * norm_w.astype(jnp.float32)).ast...]
  transfers between devices with their start and end apart: 3 -> 0, of which waited for: 3 -> 0; matrix products, arithmetic and copies ran while one was open for 1% -> 0% of each run, Pallas kernels for 0% -> 0%
where the time goes in v4:
time: 74.5 us; the launch traced here: 74.4 us
  Pallas kernels  73.2 us (98%)
  local copies, waits for them, and re-layouts  1.15 us (2%)
    pallas_call x1, Pallas kernels, per_device(): pl.pallas_call(body, out_shape=jax.ShapeDtypeStruct((tok, dim), bf), in_s...  73.2 us

profile of v4, /device:TPU:0, one launch (start us, length us, event | category | flops | bytes accessed | tf_op | source)
XLA Modules:
  0.0 74.4 jit_solution(1271347857457360549)
XLA Ops:
  0.0 73.2 %moe_layer.1 = bf16[512,1536]{1,0:T(8,128)(2,1)S(1)} custom-call(s32[4,8,128]{2,1,0:T(8,128)} %bitcast.7, bf16[512,1536]{1,0:T(8,128)(2,1)} %h_hbm.1, bf16[1536]{0:T(1024)(128)(2,1)} %nw_hbm.1, bf16[40,1536]{1,0:T(8,128)(2,1)} %bitcast.6, bf16[10,1536,128]{2,1,0:T(8,128)(2,1)} %wg_hbm.1, bf16[10,1536,128]{2,1,0:T(8,128)(2,1)} %wu_hbm.1, ...), custom_call_target="tpu_custom_call" | custom-call | tf_op jit(solution)/shard_map/moe_layer/pallas_call | solution.py:442
  73.2 1.1 %copy.9 = bf16[512,1536]{1,0:T(8,128)(2,1)} copy(bf16[512,1536]{1,0:T(8,128)(2,1)S(1)} %moe_layer.1) | data formatting | bytes 3145728

commit v5 on v4

--- a/solution.py
+++ b/solution.py
@@ -53,12 +53,14 @@
     def remote(src, dst, ssem, rsem, **where):
         return pltpu.make_async_remote_copy(src_ref=src, dst_ref=dst, send_sem=ssem, recv_sem=rsem, device_id=where, device_id_type=MESH)
 
+    first_exp = local_exp // 2 + 1
+
     def weight_copies():
         copies = []
         for e in range(local_exp):
-            copies.append(pltpu.make_async_copy(wg_hbm.at[e], wgu.at[e, :, pl.ds(0, width)], w_sem.at[0]))
-            copies.append(pltpu.make_async_copy(wu_hbm.at[e], wgu.at[e, :, pl.ds(width, width)], w_sem.at[0]))
-        copies.append(pltpu.make_async_copy(wd_hbm, wd, w_sem.at[1]))
+            copies.append(pltpu.make_async_copy(wg_hbm.at[e], wgu.at[e, :, pl.ds(0, width)], w_sem.at[e // first_exp]))
+            copies.append(pltpu.make_async_copy(wu_hbm.at[e], wgu.at[e, :, pl.ds(width, width)], w_sem.at[e // first_exp]))
+        copies.append(pltpu.make_async_copy(wd_hbm, wd, w_sem.at[2]))
         return copies
 
     def h_copy(k):
@@ -73,8 +75,13 @@
     for k in range(1, n_h):
         h_copy(k).start()
     barrier = pltpu.get_barrier_semaphore()
-    for where in ({"ep": ep_pair}, {"ep": ep_far}, {"ep": ep_diag}, {"tp": z_pair}, {"tp": z_mirror}):
+    for where in ({"ep": ep_pair}, {"ep": ep_far}, {"ep": ep_diag}, {"tp": z_pair}):
         pl.semaphore_signal(barrier, inc=1, device_id=where, device_id_type=MESH)
+
+    @pl.when(inner)
+    def _():
+        pl.semaphore_signal(barrier, inc=1, device_id={"tp": z_mirror}, device_id_type=MESH)
+
     for copy in weight_copies():
         copy.start()
 
@@ -151,7 +158,7 @@
     for b in range(N_BLK):
         norm_block(b)
         if b == 0:
-            pl.semaphore_wait(barrier, 5)
+            pl.semaphore_wait(barrier, jnp.where(inner, 5, 4))
         for u, (of, _, _) in enumerate(UNITS):
             if of == b:
                 dy(u).start()
@@ -277,29 +284,30 @@
     def each(fn, *args):
         return lambda: fn(*args)
 
-    pre = {0: [each(own_in, 0), ids_own, each(weights_in, wgu, 0)],
-           1: [each(far_in, 1), each(own_in, 1)],
+    pre = {0: [each(own_in, 0), ids_own, each(weights_in, wgu.at[pl.ds(0, first_exp)], 0)],
+           1: [each(own_in, 1), each(far_in, 1)],
            2: [ids_far, each(own_in, 2), each(far_in, 3), each(far_ready, 0)],
-           3: [each(far_in, 5), each(pair_part, 2), each(far_sum, 0), each(far_pair_in, 3),
-               each(own_in, 3), each(far_ready, 1), each(pair_part, 0), each(pair_part, 1)],
-           4: [each(whole_in, 6), each(far_pair_in, 5), each(line, (0,)), each(far_ready, 2, 3)],
-           5: [each(line, (), (0,)), each(whole_in, 7), each(far_ready, 4, 5)],
-           6: [each(line, (6,), (3,), (0,)), each(whole_pair_in, 6), each(own_in, 6)],
-           7: [each(line, (10, 11), (6, 7), (3,)), each(far_ready, 6, 7)]}
-    early = {2: [each(far_in, 4)],
-             3: [each(far_in, 6), each(far_pair_in, 4)],
-             4: [each(pair_part, 3), each(far_sum, 1), each(line, (1, 2))],
-             5: [each(pair_part, 4), each(far_sum, 2), each(far_sum, 3), each(line, (4,), (1,))],
-             6: [each(pair_part, 5), each(far_sum, 4), each(far_sum, 5), each(line, (7, 8), (4,), (1,))],
-             7: [each(pair_part, 6), each(line, (12,), (8,), (4,))]}
-    mid = {0: [each(weights_in, wd, 1), each(far_in, 0)],
+           3: [each(own_in, 3), each(far_in, 5), each(far_pair_in, 3), each(pair_part, 2), each(far_sum, 0), each(far_ready, 1), each(pair_part, 0), each(pair_part, 1)],
+           4: [each(far_pair_in, 5), each(line, (0, ), (), ()), each(far_ready, 2, 3)],
+           5: [each(whole_in, 7), each(line, (4, ), (), ()), each(far_ready, 4, 5)],
+           6: [each(own_in, 6), each(whole_pair_in, 6), each(line, (7, ), (3, ), ())],
+           7: [each(line, (11, ), (7, ), (3, )), each(far_ready, 6, 7)]}
+    early = {0: [each(weights_in, wgu.at[pl.ds(first_exp, local_exp - first_exp)], 1)],
+           2: [each(far_in, 4)],
+           3: [each(far_in, 6), each(far_pair_in, 4)],
+           4: [each(whole_in, 6), each(pair_part, 3), each(far_sum, 1), each(line, (1, 2, ), (), ())],
+           5: [each(pair_part, 4), each(far_sum, 2), each(far_sum, 3), each(line, (5, ), (0, 1, ), ())],
+           6: [each(line, (8, 9, ), (4, ), (0, ))],
+           7: [each(pair_part, 6), each(line, (12, 13, ), (8, ), (4, ))]}
+    mid = {0: [each(weights_in, wd, 2), each(far_in, 0)],
            1: [each(far_in, 2), each(far_pair_in, 0), each(far_pair_in, 1)],
            2: [each(far_pair_in, 2)],
-           4: [each(line, (3,)), each(far_pair_in, 6)],
-           5: [each(line, (5,), (2,))],
-           6: [each(line, (9,), (5,), (2,)), each(whole_pair_in, 7)],
-           7: [each(line, (13, 14), (9, 10), (5, 6))]}
+           4: [each(far_pair_in, 6), each(line, (3, ), (), ())],
+           5: [each(line, (6, ), (2, ), ())],
+           6: [each(whole_pair_in, 7), each(pair_part, 5), each(far_sum, 4), each(far_sum, 5), each(line, (10, ), (5, 6, ), (1, 2, ))],
+           7: [each(line, (14, ), (9, 10, ), (5, 6, ))]}
     out_from, join_from, lag = 15, 11, 4
+    sums_out, sums_in = 18, 18
 
     def run(tasks, step):
         for k, fns in tasks.items():
@@ -340,17 +348,25 @@
         for n in range(dim // COLS):
             pd(step, n).start()
 
+    def last_sums():
+        pair_part(7)
+        far_sum(6)
+        far_sum(7)
+
+    def pieces_from(first, sums_at, fn):
+        for b in range(first // per_blk, N_BLK):
+            stops = sorted({max(first - b * per_blk, 0), per_blk} | ({sums_at - b * per_blk} if sums_at // per_blk == b else set()))
+            for lo, hi in zip(stops, stops[1:]):
+                if b * per_blk + lo == sums_at:
+                    last_sums()
+
+                @pl.loop(lo, hi)
+                def _(i, b=b):
+                    fn(b, i)
+
     @pl.when(outer)
     def _():
-        for b in range(out_from // per_blk, N_BLK):
-            if b == 4:
-                pair_part(7)
-                far_sum(6)
-                far_sum(7)
-
-            @pl.loop(max(out_from - b * per_blk, 0), per_blk)
-            def _(i, b=b):
-                send_out(b, i)
+        pieces_from(out_from, sums_out, send_out)
 
         @pl.loop(0, n_piece)
         def _(p):
@@ -358,17 +374,11 @@
 
     @pl.when(inner)
     def _():
-        for b in range(join_from // per_blk, N_BLK):
-            if b == 4:
-                pair_part(7)
-                far_sum(6)
-                far_sum(7)
-
-            @pl.loop(max(join_from - b * per_blk, 0), per_blk)
-            def _(i, b=b):
-                join_in(b, i)
-                finish(b * per_blk + i - lag)
-
+        def step_in(b, i):
+            join_in(b, i)
+            finish(b * per_blk + i - lag)
+
+        pieces_from(join_from, sums_in, step_in)
         for p in range(n_piece - lag, n_piece):
             finish(p)
 
@@ -425,7 +435,7 @@
             pltpu.VMEM((3, N_BLK // 2, top_k, 2 * blk), jnp.int32),
             pltpu.VMEM((n_job, 2, top_k, 2 * blk), jnp.int32),
             dma((tok // (2 * blk) + 3,)),
-            dma((2,)),
+            dma((3,)),
             dma, dma((3,)),
             dma, dma((n_job,)),
             dma, dma((len(UNITS),)),

time: 74.5 us -> 73.3 us (0.984)
  Pallas kernels: 73.2 us -> 72 us
    pallas_call x1, Pallas kernels: 73.2 us -> 72 us  [per_device(): pl.pallas_call(body, out_shape=jax.ShapeDtypeStruct((tok, dim), bf), in_s...]
where the time goes in v5:
time: 73.3 us; the launch traced here: 73.1 us
  Pallas kernels  72 us (98%)
  local copies, waits for them, and re-layouts  1.15 us (2%)
    pallas_call x1, Pallas kernels, per_device(): pl.pallas_call(body, out_shape=jax.ShapeDtypeStruct((tok, dim), bf), in_s...  72 us

profile of v5, /device:TPU:0, one launch (start us, length us, event | category | flops | bytes accessed | tf_op | source)
XLA Modules:
  0.0 73.1 jit_solution(9597637374799847431)
XLA Ops:
  0.0 72.0 %moe_layer.1 = bf16[512,1536]{1,0:T(8,128)(2,1)S(1)} custom-call(s32[4,8,128]{2,1,0:T(8,128)} %bitcast.7, bf16[512,1536]{1,0:T(8,128)(2,1)} %h_hbm.1, bf16[1536]{0:T(1024)(128)(2,1)} %nw_hbm.1, bf16[40,1536]{1,0:T(8,128)(2,1)} %bitcast.6, bf16[10,1536,128]{2,1,0:T(8,128)(2,1)} %wg_hbm.1, bf16[10,1536,128]{2,1,0:T(8,128)(2,1)} %wu_hbm.1, ...), custom_call_target="tpu_custom_call" | custom-call | tf_op jit(solution)/shard_map/moe_layer/pallas_call | solution.py:452
  72.0 1.1 %copy.9 = bf16[512,1536]{1,0:T(8,128)(2,1)} copy(bf16[512,1536]{1,0:T(8,128)(2,1)S(1)} %moe_layer.1) | data formatting | bytes 3145728

commit v6 on v5

--- a/solution.py
+++ b/solution.py
@@ -20,6 +20,7 @@
     (("own", 6), ("own", 7)),
     (("far", 6), ("far", 7)),
 )
+OWN_JOBS = tuple(slot for slot, job in enumerate(JOBS) if any(kind == "own" for kind, _ in job))
 PLACE = {block: (slot, k) for slot, job in enumerate(JOBS) for k, block in enumerate(job)}
 WHOLE = 6
 UNITS = ((0, 0, 16), (0, 16, 16)) + tuple((b, 0, 32) for b in range(1, WHOLE))
@@ -116,7 +117,7 @@
         return remote(ids_ref, ids_all.at[k], ids_s, ids_r.at[k], ep=ep_to)
 
     def d1(b):
-        return remote(block("own", b), block("own", b, mine), d1_s, d1_r.at[PLACE["own", b][0]], ep=ep_pair)
+        return remote(block("own", b), block("own", b, mine), d1_s, d1_r.at[OWN_JOBS.index(PLACE["own", b][0])], ep=ep_pair)
 
     def dy(u):
         return remote(unit("own", u, side), unit("far", u, side), dy_s, dy_r.at[u], ep=ep_far)
@@ -175,7 +176,7 @@
     def own_in(slot):
         of_job = [b for kind, b in JOBS[slot] if kind == "own"]
         rows = v.at[slot, pl.ds(mine + PLACE["own", of_job[0]][1] * blk, len(of_job) * blk)]
-        remote(rows, rows, d1_s, d1_r.at[slot], ep=ep_pair).wait_recv()
+        remote(rows, rows, d1_s, d1_r.at[OWN_JOBS.index(slot)], ep=ep_pair).wait_recv()
 
     def far_in(u):
         dy(u).wait_recv()
@@ -437,7 +438,7 @@
             dma((tok // (2 * blk) + 3,)),
             dma((3,)),
             dma, dma((3,)),
-            dma, dma((n_job,)),
+            dma, dma((len(OWN_JOBS),)),
             dma, dma((len(UNITS),)),
             dma, dma((len(UNITS),)),
             dma, dma((N_BLK - WHOLE,)),

time: 73.3 us -> 73.2 us (level)
  no operation moved by 1% of the time
where the time goes in v6:
time: 73.2 us; the launch traced here: 73.1 us
  Pallas kernels  71.9 us (98%)
  local copies, waits for them, and re-layouts  1.15 us (2%)
    pallas_call x1, Pallas kernels, per_device(): pl.pallas_call(body, out_shape=jax.ShapeDtypeStruct((tok, dim), bf), in_s...  71.9 us

profile of v6, /device:TPU:0, one launch (start us, length us, event | category | flops | bytes accessed | tf_op | source)
XLA Modules:
  0.0 73.1 jit_solution(16140505394459951725)
XLA Ops:
  0.0 71.9 %moe_layer.1 = bf16[512,1536]{1,0:T(8,128)(2,1)S(1)} custom-call(s32[4,8,128]{2,1,0:T(8,128)} %bitcast.7, bf16[512,1536]{1,0:T(8,128)(2,1)} %h_hbm.1, bf16[1536]{0:T(1024)(128)(2,1)} %nw_hbm.1, bf16[40,1536]{1,0:T(8,128)(2,1)} %bitcast.6, bf16[10,1536,128]{2,1,0:T(8,128)(2,1)} %wg_hbm.1, bf16[10,1536,128]{2,1,0:T(8,128)(2,1)} %wu_hbm.1, ...), custom_call_target="tpu_custom_call" | custom-call | tf_op jit(solution)/shard_map/moe_layer/pallas_call | solution.py:453
  71.9 1.1 %copy.9 = bf16[512,1536]{1,0:T(8,128)(2,1)} copy(bf16[512,1536]{1,0:T(8,128)(2,1)S(1)} %moe_layer.1) | data formatting | bytes 3145728
